TPU v7x, 256 devices: a whole 4x4x8 slice. The times are simulated.
256 devices in a mesh: seg: 4 (over y), sub: 64 (over z, x, core).
Axes of the slice: x: 4, y: 4, z: 8, core: 2. Of those that a mesh axis runs over, the one named last changes fastest.
Arguments:
- diffusivity: float32 [256, 32768], P('seg', 'sub'), may hold values from 0.01 to 0.4
- background_flow: float32 [256, 32768], P('seg', 'sub'), may hold values from 0.5 to 2
- inlet_modes: float32 [512, 32768], P(None, 'sub'), may hold values from -0.25 to 0.25
- profile_step: float32 [512], P('sub'), may hold values from -6 to 6
- brick_owner: int32 [65536, 1], P(('seg', 'sub')), may hold values from 0 to 63; in each aligned block of 256 rows (0 to 255, 256 to 511, ...) at most 8 rows name the same one
- voxel_row: int32 [65536], P(('seg', 'sub')), may hold values from 0 to 15
- noise_weight: float32 [4096, 128], P(('seg', 'sub')), may hold values from 0.1 to 10
- spread_matrix: float32 [128, 128], replicated, may hold values from -0.5 to 0.5
Outputs:
- forward_field: float32 [256, 32768], P('seg', 'sub')
- response: float32 [4096, 128], P(('seg', 'sub'))
- product: float32 [512], P(('seg', 'sub'))
Inputs may be any that keep to these rules, and one draw needn't show every extreme that they name: `brick_owner`: among the 256 blocks of one device each brick index is named at most 8 times, and exactly 8 times on some device; blocks go to bricks of their own segment group.
All inputs are finite; a program needn't handle non-finite values.
Results may differ from a plain program's by a relative error of at most 0.00019.
Values sent between devices are 32-bit elements; how exact they have to be, the bound alone decides.
No kernel may reach another device: no remote copies, remote signals or barrier semaphores. Data moves between devices by JAX's collectives and lax.ppermute only.
A program may use at most 128 MiB of HBM per device.

v0:
```python
import jax
import jax.numpy as jnp
from jax import lax
from jax.experimental import pallas as pl
from jax.experimental.pallas import tpu as pltpu
from jax.sharding import PartitionSpec as P

SIGMA = 0.001
HIGH = lax.Precision.HIGHEST
BF = jnp.bfloat16
F32 = jnp.float32
HALO = 12
PAIRS = 76
T = 32
TC = 16
SLOTS = 8
VROWS = 16
ALL = ("seg", "sub")


def split3(x):
    hi = x.astype(BF)
    rest = x - hi.astype(F32)
    mid = rest.astype(BF)
    lo = (rest - mid.astype(F32)).astype(BF)
    return hi, mid, lo


def select_dot(x, chosen):
    hi, mid, lo = split3(x)
    out = jnp.dot(lo, chosen, preferred_element_type=F32)
    out = out + jnp.dot(mid, chosen, preferred_element_type=F32)
    return out + jnp.dot(hi, chosen, preferred_element_type=F32)


def lane(shape):
    return lax.broadcasted_iota(jnp.int32, shape, len(shape) - 1)


def sub(shape):
    return lax.broadcasted_iota(jnp.int32, shape, len(shape) - 2)


def to_pairs_matrix(offset):
    n = lane((256, 256))
    pair = jnp.where(n < 128, n, n - 128)
    x = 2 * pair + jnp.where(n < 128, 0, 1)
    source = jnp.where(
        x < HALO,
        128 + offset + x,
        jnp.where(x < HALO + 128, x - HALO, 128 + offset + x - 128),
    )
    hit = (source == sub((256, 256))) & (pair < PAIRS)
    return jnp.where(hit, 1.0, 0.0).astype(BF)


def from_pairs_matrix():
    row = sub((256, 128))
    y = lane((256, 128))
    source = (y >> 1) + HALO // 2 + jnp.where((y & 1) == 1, 128, 0)
    return jnp.where(source == row, 1.0, 0.0).astype(BF)


def edge_tile(tile_low, tile_high, shift):
    n = lane(tile_low.shape)
    base = shift - HALO
    low = jnp.where((n >= base) & (n < base + HALO), pltpu.roll(tile_low, shift, 1), 0.0)
    high = jnp.where(
        (n >= shift) & (n < shift + HALO), pltpu.roll(tile_high, shift, 1), 0.0
    )
    return low, high


def edges_kernel(k_ref, f_ref, up_ref, down_ref):
    kl, kh = edge_tile(k_ref[:, 384:512], k_ref[:, 0:128], HALO)
    fl, fh = edge_tile(f_ref[:, 384:512], f_ref[:, 0:128], 3 * HALO)
    up_ref[...] = kl + fl
    down_ref[...] = kh + fh


def spread_kernel(k_ref, f_ref, low_ref, high_ref, out_ref):
    for q in range(4):
        out_ref[q, 0] = k_ref[:, 128 * q : 128 * q + 128]
        out_ref[q, 1] = f_ref[:, 128 * q : 128 * q + 128]
        below = max(q - 1, 0)
        above = min(q + 1, 3)
        kl, kh = edge_tile(
            k_ref[:, 128 * below : 128 * below + 128],
            k_ref[:, 128 * above : 128 * above + 128],
            HALO,
        )
        fl, fh = edge_tile(
            f_ref[:, 128 * below : 128 * below + 128],
            f_ref[:, 128 * above : 128 * above + 128],
            3 * HALO,
        )
        low = low_ref[...] if q == 0 else kl + fl
        high = high_ref[...] if q == 3 else kh + fh
        out_ref[q, 2] = low + high


def profile_kernel(step_ref, modes_ref, out_ref):
    steps = step_ref[...]
    total = jnp.zeros((64, 128), F32)
    for j in range(8):
        total = total + steps[:, j : j + 1] * modes_ref[pl.ds(j, 64, stride=8), :]
    out_ref[0] = jnp.broadcast_to(jnp.sum(total, axis=0, keepdims=True), (8, 128))


def shifted(x, amount):
    n = sub(x.shape)
    if amount > 0:
        return jnp.where(n >= amount, pltpu.roll(x, amount, 0), 0.0)
    return jnp.where(n < 8 + amount, pltpu.roll(x, 8 + amount, 0), 0.0)


class Level:
    def __init__(self, gains, prefix, partial, count, forward):
        self.gains, self.prefix, self.partial = gains, prefix, partial
        self.count, self.forward = count, forward
        self.order = range(count) if forward else range(count - 1, -1, -1)

    def prepare(self, parts):
        one = 1 if self.forward else -1
        self.steps = []
        for p in range(parts):
            running = None
            for t in self.order:
                g = self.gains[p, t]
                running = g if running is None else running * g
                self.prefix[p, t] = running
            a = shifted(running, one)
            steps = []
            for d in (1, 2, 4):
                steps.append(a)
                a = a * shifted(a, one * d)
            self.steps.append(steps)

    def scan(self, parts, driving, emit):
        one = 1 if self.forward else -1
        running = [None] * parts
        for t in self.order:
            xs = driving(t)
            for p in range(parts):
                y = xs[p]
                if running[p] is not None:
                    y = self.gains[p, t] * running[p] + y
                running[p] = y
                self.partial[p, t] = y
        carry = []
        for p in range(parts):
            b = shifted(running[p], one)
            for d, a in zip((1, 2, 4), self.steps[p]):
                b = b + a * shifted(b, one * d)
            carry.append(b)
        for t in self.order:
            emit(t, [self.partial[p, t] + self.prefix[p, t] * carry[p] for p in range(parts)])


def beside(ref, t, count, forward, p):
    if forward:
        return ref[p, t + 1] if t + 1 < count else shifted(ref[p, 0], -1)
    return ref[p, t - 1] if t > 0 else shifted(ref[p, count - 1], 1)


def fine_sum(ref, t, forward):
    even, odd = ref[0, t], ref[1, t]
    return (
        beside(ref, t, T, forward, 0) + odd + pltpu.roll(odd, 1, 1),
        beside(ref, t, T, forward, 1) + even + pltpu.roll(even, 127, 1),
    )


def coarse_sum(ref, t, forward):
    own = ref[0, t]
    return beside(ref, t, TC, forward, 0) + pltpu.roll(own, 1, 1) + pltpu.roll(own, 127, 1)


SOLVE_SCRATCH = [
    pltpu.VMEM((2, T, 8, 128), F32),
    pltpu.VMEM((2, T, 8, 128), F32),
    pltpu.VMEM((2, T, 8, 128), F32),
    pltpu.VMEM((2, T, 8, 128), F32),
    pltpu.VMEM((2, T, 8, 128), F32),
    pltpu.VMEM((2, T, 8, 128), F32),
    pltpu.VMEM((1, TC, 8, 128), F32),
    pltpu.VMEM((1, TC, 8, 128), F32),
    pltpu.VMEM((1, TC, 8, 128), F32),
    pltpu.VMEM((1, TC, 8, 128), F32),
    pltpu.VMEM((1, TC, 8, 128), F32),
    pltpu.VMEM((1, TC, 8, 128), F32),
    pltpu.VMEM((1, TC, 8, 128), F32),
]


def solve_on_slab(kf, source, scratch, forward, finish):
    (gains, prefix, partial, scale, field, kept, cgains, cprefix, cpartial, cscale, ck, cfield,
     csource) = scratch
    for c in range(TC):
        ksum = fsum = None
        for t in (2 * c, 2 * c + 1):
            for p in range(2):
                k, f = kf[p, t], kf[2 + p, t]
                inverse = 1.0 / (4.0 * k + f + SIGMA)
                if forward:
                    gains[p, t] = (k + f) * inverse
                    scale[p, t] = k * inverse
                else:
                    if t + 1 < T:
                        up = kf[p, t + 1] + kf[2 + p, t + 1]
                    else:
                        up = shifted(kf[p, 0] + kf[2 + p, 0], -1)
                    gains[p, t] = up * inverse
                    scale[p, t] = inverse
                ksum = k if ksum is None else ksum + k
                fsum = f if fsum is None else fsum + f
        kc = 0.25 * ksum
        fc = 0.5 * fsum
        inverse = 1.0 / (4.0 * kc + fc + 4.0 * SIGMA)
        ck[0, c] = kc
        cfield[0, c] = kc + fc
        cscale[0, c] = inverse
    for c in range(TC):
        if forward:
            cgains[0, c] = cfield[0, c] * cscale[0, c]
        else:
            up = cfield[0, c + 1] if c + 1 < TC else shifted(cfield[0, 0], -1)
            cgains[0, c] = up * cscale[0, c]
    fine = Level(gains, prefix, partial, T, forward)
    fine.prepare(2)
    coarse = Level(cgains, cprefix, cpartial, TC, forward)
    coarse.prepare(1)

    def keep_fine(t, values):
        for p in range(2):
            field[p, t] = values[p] if forward else kf[p, t] * values[p]

    def correct(residual):
        for c in range(TC):
            total = None
            for t in (2 * c, 2 * c + 1):
                for part in residual(t):
                    total = part if total is None else total + part
            csource[0, c] = total * cscale[0, c]

        def keep_first(c, values):
            cfield[0, c] = values[0] if forward else ck[0, c] * values[0]

        coarse.scan(1, lambda c: (csource[0, c],), keep_first)

        def second(c):
            total = coarse_sum(cfield, c, forward)
            if forward:
                total = ck[0, c] * total
            return (csource[0, c] + cscale[0, c] * total,)

        def add_back(c, values):
            for t in (2 * c, 2 * c + 1):
                for p in range(2):
                    more = values[0] if forward else kf[p, t] * values[0]
                    field[p, t] = field[p, t] + more

        coarse.scan(1, second, add_back)

    def relaxed(t):
        sums = fine_sum(field, t, forward)
        start = source(t)
        return tuple(
            scale[p, t] * sums[p] if start is None else start[p] + scale[p, t] * sums[p]
            for p in range(2)
        )

    def started(t):
        start = source(t)
        return (jnp.zeros((8, 128), F32),) * 2 if start is None else start

    def residual_first(t):
        sums = fine_sum(field, t, forward)
        return tuple(kf[p, t] * sums[p] if forward else sums[p] for p in range(2))

    def relaxed_kept(t):
        sums = fine_sum(field, t, forward)
        start = source(t)
        for p in range(2):
            kept[p, t] = sums[p]
        return tuple(
            scale[p, t] * sums[p] if start is None else start[p] + scale[p, t] * sums[p]
            for p in range(2)
        )

    def residual_second(t):
        sums = fine_sum(field, t, forward)
        parts = tuple(sums[p] - kept[p, t] for p in range(2))
        return tuple(kf[p, t] * parts[p] if forward else parts[p] for p in range(2))

    fine.scan(2, started, keep_fine)
    correct(residual_first)
    fine.scan(2, relaxed, keep_fine)
    fine.scan(2, relaxed_kept, keep_fine)
    correct(residual_second)
    fine.scan(2, relaxed, finish)


def forward_kernel(place_ref, in_ref, own_ref, near_ref, out_ref, kf_ref, natural, *scratch):
    for field in range(2):
        chosen = to_pairs_matrix(2 * HALO * field)
        for g in range(4):
            x = jnp.concatenate([in_ref[g, field], in_ref[g, 2]], axis=1)
            got = select_dot(x, chosen)
            natural[0, 64 * g : 64 * g + 64] = got[:, :128]
            natural[1, 64 * g : 64 * g + 64] = got[:, 128:]
        for p in range(2):
            for t in range(T):
                kf_ref[2 * field + p, t] = natural[p, pl.ds(t, 8, stride=T), :]
    q = place_ref[0]
    low = jnp.where(q == 0, near_ref[3], own_ref[jnp.maximum(q - 1, 0)])
    high = jnp.where(q == 3, near_ref[0], own_ref[jnp.minimum(q + 1, 3)])
    parts = edge_tile(low, high, HALO)
    profile = select_dot(
        jnp.concatenate([own_ref[q], parts[0] + parts[1]], axis=1), to_pairs_matrix(0)
    )
    profile = jnp.where(sub((8, 256)) == 0, profile, 0.0)
    begin = []
    for p in range(2):
        k, f = kf_ref[p, 0], kf_ref[2 + p, 0]
        begin.append((k + f) * profile[:, 128 * p : 128 * p + 128] / (4.0 * k + f + SIGMA))
    result = scratch[2]

    def finish(t, values):
        for p in range(2):
            result[p, t] = values[p]

    solve_on_slab(kf_ref, lambda t: tuple(begin) if t == 0 else None, scratch, True, finish)
    chosen = from_pairs_matrix()
    both = jnp.concatenate(
        [result[0].reshape(256, 128), result[1].reshape(256, 128)], axis=1
    )
    got = select_dot(both, chosen)
    for t in range(T):
        out_ref[pl.ds(t, 8, stride=T), :] = got[8 * t : 8 * t + 8]


def pack_kernel(slot_ref, in_ref, field_ref, out_ref):
    for q in range(4):
        field_ref[:, 128 * q : 128 * q + 128] = in_ref[q]
    out_ref[...] = jnp.zeros(out_ref.shape, F32)
    for i in range(256):
        out_ref[pl.ds(slot_ref[i], 1), :] = in_ref[i // 64, i % 64 : i % 64 + 1]


def voxel_kernel(in_ref, row_ref, weight_ref, spread_ref, response_ref, out_ref):
    rows = jnp.broadcast_to(row_ref[...], (VROWS, 512))
    mask = jnp.where(rows == sub((VROWS, 512)).astype(F32), 1.0, 0.0)
    hi, mid, lo = split3(in_ref[...])
    chosen = mask.astype(BF)
    voxels = jnp.dot(chosen, lo, preferred_element_type=F32)
    voxels = voxels + jnp.dot(chosen, mid, preferred_element_type=F32)
    voxels = voxels + jnp.dot(chosen, hi, preferred_element_type=F32)
    spread = spread_ref[...]
    response = lax.dot_general(
        voxels, spread, (((1,), (1,)), ((), ())), precision=HIGH, preferred_element_type=F32
    )
    response_ref[...] = response
    weighted = jnp.dot(
        weight_ref[...] * response, spread, precision=HIGH, preferred_element_type=F32
    )
    back = jnp.transpose(mask).astype(BF)
    total = None
    for part in reversed(split3(weighted)):
        got = jnp.dot(back, part, preferred_element_type=F32)
        total = got if total is None else total + got
    out_ref[...] = total


def unpack_kernel(slot_ref, in_ref, out_ref, up_ref, down_ref):
    for i in range(256):
        out_ref[i // 64, i % 64 : i % 64 + 1] = in_ref[pl.ds(slot_ref[i], 1), :]
    low, high = edge_tile(out_ref[3], out_ref[0], HALO)
    up_ref[...] = low
    down_ref[...] = high


def driving_kernel(in_ref, low_ref, high_ref, out_ref):
    for q in range(4):
        out_ref[q, 0] = in_ref[q]
        low, high = edge_tile(in_ref[max(q - 1, 0)], in_ref[min(q + 1, 3)], HALO)
        if q == 0:
            low = low_ref[...]
        if q == 3:
            high = high_ref[...]
        out_ref[q, 1] = low + high


def adjoint_kernel(place_ref, in_ref, kf_ref, modes_ref, out_ref, natural, begin, *scratch):
    chosen = to_pairs_matrix(0)
    for g in range(4):
        x = jnp.concatenate([in_ref[g, 0], in_ref[g, 1]], axis=1)
        got = select_dot(x, chosen)
        natural[0, 64 * g : 64 * g + 64] = got[:, :128]
        natural[1, 64 * g : 64 * g + 64] = got[:, 128:]
    for p in range(2):
        for t in range(T):
            k, f = kf_ref[p, t], kf_ref[2 + p, t]
            begin[p, t] = natural[p, pl.ds(t, 8, stride=T), :] / (4.0 * k + f + SIGMA)
    flux = []

    def finish(t, values):
        if t == 0:
            for p in range(2):
                flux.append((kf_ref[p, 0] + kf_ref[2 + p, 0]) * values[p])

    solve_on_slab(kf_ref, lambda t: (begin[0, t], begin[1, t]), scratch, False, finish)
    natural_flux = select_dot(jnp.concatenate(flux, axis=1), from_pairs_matrix())
    row = natural_flux[0:1]
    out = jnp.zeros((256, 128), F32)
    for j in range(2):
        part = jnp.sum(modes_ref[pl.ds(j, 256, stride=2), :] * row, axis=1, keepdims=True)
        out = jnp.where(lane((256, 128)) == j, part, out)
    out_ref[...] = out


VM = pl.BlockSpec(memory_space=pltpu.VMEM)
SM = pl.BlockSpec(memory_space=pltpu.SMEM)


def shape(*dims):
    return jax.ShapeDtypeStruct(dims, F32)


def exchange(array, axis):
    return lax.all_to_all(array, axis, split_axis=0, concat_axis=0, tiled=True)


def on_device(
    diffusivity,
    background_flow,
    inlet_modes,
    profile_step,
    brick_owner,
    voxel_row,
    noise_weight,
    spread_matrix,
):
    count = lax.axis_size("sub")
    place = lax.axis_index("seg").astype(jnp.int32).reshape(1)
    up = [(i, i + 1) for i in range(count - 1)]
    down = [(i + 1, i) for i in range(count - 1)]

    to_up, to_down = pl.pallas_call(
        edges_kernel, out_shape=(shape(64, 128), shape(64, 128)), name="edges"
    )(diffusivity, background_flow)
    low = lax.ppermute(to_up, "sub", up)
    high = lax.ppermute(to_down, "sub", down)

    owners = brick_owner.reshape(64, 4).T.reshape(256)
    rows = voxel_row.reshape(64, 4).T.reshape(256)
    index = jnp.arange(256, dtype=jnp.int32)
    earlier = (owners[:, None] == owners[None, :]) & (index[:, None] < index[None, :])
    slots = owners * SLOTS + jnp.sum(earlier.astype(jnp.int32), axis=0)
    named = slots[:, None] == jnp.arange(count * SLOTS, dtype=jnp.int32)[None, :]
    slot_rows = VROWS - jnp.sum(jnp.where(named, VROWS - rows[:, None], 0), axis=0)
    message = jnp.concatenate(
        [
            jnp.broadcast_to(profile_step[None, :], (count, 8)),
            slot_rows.reshape(count, SLOTS).astype(F32),
            jnp.zeros((count, 112), F32),
        ],
        axis=1,
    )
    heard = exchange(message.reshape(count, 1, 128), "sub").reshape(count, 128)
    heard_rows = heard[:, 8:16].reshape(1, count * SLOTS)

    own_profile = pl.pallas_call(
        profile_kernel,
        grid=(4,),
        in_specs=[
            pl.BlockSpec((64, 128), lambda c: (0, 0)),
            pl.BlockSpec((512, 128), lambda c: (0, c)),
        ],
        out_specs=pl.BlockSpec((1, 8, 128), lambda c: (c, 0, 0)),
        out_shape=shape(4, 8, 128),
        name="profile",
    )(heard, inlet_modes)
    ends = [(i, i + 1) for i in range(count - 1)]
    ends += [(3 * count + i + 1, 3 * count + i) for i in range(count - 1)]
    near_profile = lax.ppermute(own_profile, ALL, ends)

    spread = pl.pallas_call(
        spread_kernel, out_shape=shape(4, 3, 64, 128), name="spread"
    )(diffusivity, background_flow, low, high)
    slab = exchange(spread, "seg")

    field, kf = pl.pallas_call(
        forward_kernel,
        in_specs=[SM, VM, VM, VM],
        out_shape=(shape(256, 128), shape(4, T, 8, 128)),
        scratch_shapes=[pltpu.VMEM((2, 256, 128), F32)] + SOLVE_SCRATCH,
        name="forward",
    )(place, slab, own_profile, near_profile)
    back = exchange(field.reshape(4, 64, 128), "seg")

    forward_field, packed = pl.pallas_call(
        pack_kernel,
        in_specs=[SM, VM],
        out_shape=(shape(64, 512), shape(count * SLOTS, 128)),
        name="pack",
    )(slots, back)
    arrived = exchange(packed.reshape(count, SLOTS, 128), "sub")

    response, answer = pl.pallas_call(
        voxel_kernel,
        out_shape=(shape(VROWS, 128), shape(count * SLOTS, 128)),
        name="voxels",
    )(arrived.reshape(count * SLOTS, 128), heard_rows, noise_weight, spread_matrix)
    answered = exchange(answer.reshape(count, SLOTS, 128), "sub")

    driving, to_up, to_down = pl.pallas_call(
        unpack_kernel,
        in_specs=[SM, VM],
        out_shape=(shape(4, 64, 128), shape(64, 128), shape(64, 128)),
        name="unpack",
    )(slots, answered.reshape(count * SLOTS, 128))
    low = lax.ppermute(to_up, "sub", up)
    high = lax.ppermute(to_down, "sub", down)
    spread = pl.pallas_call(
        driving_kernel, out_shape=shape(4, 2, 64, 128), name="driving"
    )(driving, low, high)
    slab = exchange(spread, "seg")

    partial = pl.pallas_call(
        adjoint_kernel,
        grid_spec=pltpu.PrefetchScalarGridSpec(
            num_scalar_prefetch=1,
            grid=(1,),
            in_specs=[
                pl.BlockSpec((4, 2, 64, 128), lambda i, q: (0, 0, 0, 0)),
                pl.BlockSpec((4, T, 8, 128), lambda i, q: (0, 0, 0, 0)),
                pl.BlockSpec((512, 128), lambda i, q: (0, q[0])),
            ],
            out_specs=pl.BlockSpec((256, 128), lambda i, q: (0, 0)),
            scratch_shapes=[
                pltpu.VMEM((2, 256, 128), F32),
                pltpu.VMEM((2, T, 8, 128), F32),
            ]
            + SOLVE_SCRATCH,
        ),
        out_shape=shape(256, 128),
        name="adjoint",
    )(place, slab, kf, inlet_modes)
    gathered = exchange(partial.reshape(256, 1, 128), ALL)
    product = jnp.sum(gathered, axis=(0, 1))[:2]
    return (forward_field, response, product)


def solution(mesh):
    in_specs = (
        P("seg", "sub"),
        P("seg", "sub"),
        P(None, "sub"),
        P("sub"),
        P(ALL, None),
        P(ALL),
        P(ALL, None),
        P(),
    )
    out_specs = (P("seg", "sub"), P(ALL, None), P(ALL))
    return jax.shard_map(
        on_device, mesh=mesh, in_specs=in_specs, out_specs=out_specs, check_vma=False
    )
```

profile of v0, /device:TPU:1, one launch (start us, length us, event | category | flops | bytes accessed | tf_op | source)
XLA Modules:
  0.0 159.4 jit_solution(9534366365220089558)
XLA Ops:
  0.6 0.7 pad.clone
  1.3 0.0 copy-start.10
  1.3 0.1 pad.2.clone
  1.4 0.6 copy-done.10
  2.0 0.1 sub.31
  2.1 0.1 copy.17
  2.2 0.1 sub.33
  2.2 0.0 copy-start.11
  2.2 0.5 broadcast.26
  2.8 0.2 copy-done.11
  2.9 0.7 reduce.3
  3.6 0.1 reshape.70
  3.7 0.1 copy.16
  3.8 0.1 reshape.71
  3.9 0.1 convert_reduce_fusion
  4.0 0.0 copy-start.8
  4.0 0.1 select_reduce_fusion
  4.2 0.4 copy-done.8
  4.6 0.1 convert_element_type.11
  4.7 0.7 maximum_maximum_fusion
  5.4 13.0 %all-to-all-start.1 = ((f32[64,1,128]{2,1,0:T(1,128)}), f32[64,1,128]{2,1,0:T(1,128)S(1)}, u32[]{:S(2)}, u32[]{:S(2)}) async-start(f32[64,1,128]{2,1,0:T(1,128)} %bitcast.3), calls=%async_computation.1 | async-start | bytes 65536 | tf_op jit(solution)/shard_map/all_to_all | solution.py:431
  18.4 1.7 %edges.1 = (f32[64,128]{1,0:T(8,128)}, f32[64,128]{1,0:T(8,128)}) custom-call(f32[64,512]{1,0:T(8,128)} %k_ref.3, f32[64,512]{1,0:T(8,128)} %f_ref.3), custom_call_target="tpu_custom_call" | custom-call | tf_op jit(solution)/shard_map/edges/pallas_call | solution.py:449
  20.0 3.5 %collective-permute-start = (f32[64,128]{1,0:T(8,128)}, f32[64,128]{1,0:T(8,128)S(1)}, u32[]{:S(2)}, u32[]{:S(2)}) collective-permute-start(f32[64,128]{1,0:T(8,128)} %get-tuple-element.14), channel_id=1, source_target_pairs={{0,1},{1,2},{2,3},{3,4},{4,5},{5,6},{6,7},{7,8},{8,9},{9,10},{10,1... | collective-permute-start | bytes 98312 | tf_op jit(solution)/shard_map/ppermute | solution.py:452
  23.6 1.9 %collective-permute-start.1 = (f32[64,128]{1,0:T(8,128)}, f32[64,128]{1,0:T(8,128)S(1)}, u32[]{:S(2)}, u32[]{:S(2)}) collective-permute-start(f32[64,128]{1,0:T(8,128)} %get-tuple-element.15), channel_id=1, source_target_pairs={{1,0},{2,1},{3,2},{4,3},{5,4},{6,5},{7,6},{8,7},{9,8},{10,9},{11,1... | collective-permute-start | bytes 98312 | tf_op jit(solution)/shard_map/ppermute | solution.py:453
  25.5 0.0 collective-permute-done.low_ref
  25.5 0.0 copy-start.6
  25.5 3.5 %collective-permute-done.1.high_ref = f32[64,128]{1,0:T(8,128)S(1)} collective-permute-done((f32[64,128]{1,0:T(8,128)}, f32[64,128]{1,0:T(8,128)S(1)}, u32[]{:S(2)}, u32[]{:S(2)}) %collective-permute-start.1) | collective-permute-done | bytes 32800 | tf_op jit(solution)/shard_map/ppermute | solution.py:453
  29.0 0.0 copy-done.6
  29.0 0.0 copy-start.7
  29.0 0.6 copy-done.7
  29.6 1.9 %spread.1 = f32[4,3,64,128]{3,2,1,0:T(8,128)} custom-call(f32[64,512]{1,0:T(8,128)} %k_ref.3, f32[64,512]{1,0:T(8,128)} %f_ref.3, f32[64,128]{1,0:T(8,128)} %copy-done.6, f32[64,128]{1,0:T(8,128)} %copy-done.7), custom_call_target="tpu_custom_call" | custom-call | tf_op jit(solution)/shard_map/spread/pallas_call | solution.py:488
  31.5 0.0 all-to-all-done.1
  31.5 0.6 copy-done.2
  32.1 4.2 %all-to-all-start = ((f32[4,3,64,128]{3,2,1,0:T(8,128)}), f32[4,3,64,128]{3,2,1,0:T(8,128)S(1)}, u32[]{:S(2)}, u32[]{:S(2)}) async-start(f32[4,3,64,128]{3,2,1,0:T(8,128)} %spread.1), calls=%async_computation | async-start | bytes 786432 | tf_op jit(solution)/shard_map/all_to_all | solution.py:431
  36.3 3.4 %profile.1.own_ref = f32[4,8,128]{2,1,0:T(8,128)} custom-call(f32[64,128]{1,0:T(8,128)} %bitcast.18, f32[512,512]{1,0:T(8,128)} %modes_ref.3), custom_call_target="tpu_custom_call" | custom-call | tf_op jit(solution)/shard_map/profile/pallas_call | solution.py:473
  39.7 2.3 %collective-permute-start.2 = (f32[4,8,128]{2,1,0:T(8,128)}, f32[4,8,128]{2,1,0:T(8,128)S(1)}, u32[]{:S(2)}, u32[]{:S(2)}) collective-permute-start(f32[4,8,128]{2,1,0:T(8,128)} %profile.1.own_ref), channel_id=1, source_target_pairs={{0,1},{1,2},{2,3},{3,4},{4,5},{5,6},{6,7},{7,8},{8,9},{9,10},{10,1... | collective-permute-start | bytes 49160 | tf_op jit(solution)/shard_map/ppermute | solution.py:486
  42.0 1.1 collective-permute-done.2.near_ref
  43.1 0.2 all-to-all-done.in_ref
  43.3 0.4 copy-done.9
  43.7 0.3 copy-done
  44.0 4.0 %forward.1 = (f32[256,128]{1,0:T(8,128)}, f32[4,32,8,128]{3,2,1,0:T(8,128)}) custom-call(s32[1]{0:T(128)} %bitcast.1.place_ref, f32[4,3,64,128]{3,2,1,0:T(8,128)} %copy-done, f32[4,8,128]{2,1,0:T(8,128)} %profile.1.own_ref, f32[4,8,128]{2,1,0:T(8,128)} %copy-done.9), custom_call_target="tpu_custom_call" | custom-call | tf_op jit(solution)/shard_map/forward/pallas_call | solution.py:493
  48.0 10.6 %all_to_all.35.in_ref = f32[4,64,128]{2,1,0:T(8,128)} all-to-all(f32[4,64,128]{2,1,0:T(8,128)} %bitcast.22), channel_id=1, replica_groups=mesh['seg'=4,'sub'=64] {'seg'}, dimensions={0} | all-to-all | bytes 262144 | tf_op jit(solution)/shard_map/all_to_all | solution.py:431
  58.6 1.8 %pack.1 = (f32[64,512]{1,0:T(8,128)}, f32[512,128]{1,0:T(8,128)}) custom-call(s32[256]{0:T(256)} %copy-done.8, f32[4,64,128]{2,1,0:T(8,128)} %all_to_all.35.in_ref), custom_call_target="tpu_custom_call" | custom-call | tf_op jit(solution)/shard_map/pack/pallas_call | solution.py:502
  60.4 15.4 %all-to-all-start.3 = ((f32[64,8,128]{2,1,0:T(8,128)}), f32[64,8,128]{2,1,0:T(8,128)S(1)}, u32[]{:S(2)}, u32[]{:S(2)}) async-start(f32[64,8,128]{2,1,0:T(8,128)} %bitcast.20), calls=%async_computation.3 | async-start | bytes 524288 | tf_op jit(solution)/shard_map/all_to_all | solution.py:431
  75.8 0.0 copy-done.3
  75.9 0.1 slice.8
  75.9 0.7 reshape.78.row_ref
  76.6 12.3 %all-to-all-done.3 = f32[64,8,128]{2,1,0:T(8,128)S(1)} async-done(((f32[64,8,128]{2,1,0:T(8,128)}), f32[64,8,128]{2,1,0:T(8,128)S(1)}, u32[]{:S(2)}, u32[]{:S(2)}) %all-to-all-start.3) | async-done | bytes 262176 | tf_op jit(solution)/shard_map/all_to_all | solution.py:431
  88.9 0.7 copy-done.1
  89.6 2.6 %voxels.1 = (f32[16,128]{1,0:T(8,128)}, f32[512,128]{1,0:T(8,128)}) custom-call(f32[512,128]{1,0:T(8,128)} %bitcast.15, f32[1,512]{1,0:T(1,128)} %reshape.78.row_ref, f32[16,128]{1,0:T(8,128)} %weight_ref.1, f32[128,128]{1,0:T(8,128)} %spread_ref.1), custom_call_target="tpu_custom_call" | custom-call | tf_op jit(solution)/shard_map/voxels/pallas_call | solution.py:510
  92.3 18.2 %all_to_all.36 = f32[64,8,128]{2,1,0:T(8,128)} all-to-all(f32[64,8,128]{2,1,0:T(8,128)} %bitcast.21), channel_id=1, replica_groups=mesh['seg'=4,'sub'=64] {'sub'}, dimensions={0} | all-to-all | bytes 524288 | tf_op jit(solution)/shard_map/all_to_all | solution.py:431
  110.5 1.8 %unpack.1 = (f32[4,64,128]{2,1,0:T(8,128)}, f32[64,128]{1,0:T(8,128)}, f32[64,128]{1,0:T(8,128)}) custom-call(s32[256]{0:T(256)} %copy-done.8, f32[512,128]{1,0:T(8,128)} %bitcast.16), custom_call_target="tpu_custom_call" | custom-call | tf_op jit(solution)/shard_map/unpack/pallas_call | solution.py:517
  112.3 2.7 %collective-permute-start.3 = (f32[64,128]{1,0:T(8,128)}, f32[64,128]{1,0:T(8,128)S(1)}, u32[]{:S(2)}, u32[]{:S(2)}) collective-permute-start(f32[64,128]{1,0:T(8,128)} %get-tuple-element.22), channel_id=1, source_target_pairs={{0,1},{1,2},{2,3},{3,4},{4,5},{5,6},{6,7},{7,8},{8,9},{9,10},{10,1... | collective-permute-start | bytes 98312 | tf_op jit(solution)/shard_map/ppermute | solution.py:523
  115.0 1.9 %collective-permute-start.4 = (f32[64,128]{1,0:T(8,128)}, f32[64,128]{1,0:T(8,128)S(1)}, u32[]{:S(2)}, u32[]{:S(2)}) collective-permute-start(f32[64,128]{1,0:T(8,128)} %get-tuple-element.23), channel_id=1, source_target_pairs={{1,0},{2,1},{3,2},{4,3},{5,4},{6,5},{7,6},{8,7},{9,8},{10,9},{11,1... | collective-permute-start | bytes 98312 | tf_op jit(solution)/shard_map/ppermute | solution.py:524
  116.9 0.0 collective-permute-done.3.low_ref
  116.9 0.0 copy-start.4
  116.9 3.5 %collective-permute-done.4.high_ref = f32[64,128]{1,0:T(8,128)S(1)} collective-permute-done((f32[64,128]{1,0:T(8,128)}, f32[64,128]{1,0:T(8,128)S(1)}, u32[]{:S(2)}, u32[]{:S(2)}) %collective-permute-start.4) | collective-permute-done | bytes 32800 | tf_op jit(solution)/shard_map/ppermute | solution.py:524
  120.4 0.0 copy-done.4
  120.4 0.6 copy-done.5
  121.0 1.8 %driving.1 = f32[4,2,64,128]{3,2,1,0:T(8,128)} custom-call(f32[4,64,128]{2,1,0:T(8,128)} %get-tuple-element.21.in_ref, f32[64,128]{1,0:T(8,128)} %copy-done.4, f32[64,128]{1,0:T(8,128)} %copy-done.5), custom_call_target="tpu_custom_call" | custom-call | tf_op jit(solution)/shard_map/driving/pallas_call | solution.py:525
  122.8 9.6 %all_to_all.37.in_ref = f32[4,2,64,128]{3,2,1,0:T(8,128)} all-to-all(f32[4,2,64,128]{3,2,1,0:T(8,128)} %driving.1), channel_id=1, replica_groups=mesh['seg'=4,'sub'=64] {'seg'}, dimensions={0} | all-to-all | bytes 524288 | tf_op jit(solution)/shard_map/all_to_all | solution.py:431
  132.4 3.8 %adjoint.1 = f32[256,128]{1,0:T(8,128)} custom-call(s32[1]{0:T(128)} %bitcast.1.place_ref, f32[4,2,64,128]{3,2,1,0:T(8,128)} %all_to_all.37.in_ref, f32[4,32,8,128]{3,2,1,0:T(8,128)} %get-tuple-element.24.kf_ref, f32[512,512]{1,0:T(8,128)} %modes_ref.3), custom_call_target="tpu_custom_call" | custom-call | tf_op jit(solution)/shard_map/adjoint/pallas_call | solution.py:530
  136.2 22.4 %all_to_all.38 = f32[256,1,128]{2,1,0:T(1,128)S(1)} all-to-all(f32[256,1,128]{2,1,0:T(1,128)} %bitcast.17), channel_id=1, replica_groups=mesh['seg'=4,'sub'=64] {'seg','sub'}, dimensions={0} | all-to-all | bytes 262144 | tf_op jit(solution)/shard_map/all_to_all | solution.py:431
  158.6 0.8 reduce_sum.29
  (10 shorter events, 0.0 us)
Async XLA Ops:
  1.3 0.7 copy-start.10
  2.2 0.7 copy-start.11
  4.0 0.6 copy-start.8
  5.4 26.2 %all-to-all-start.1 = ((f32[64,1,128]{2,1,0:T(1,128)}), f32[64,1,128]{2,1,0:T(1,128)S(1)}, u32[]{:S(2)}, u32[]{:S(2)}) async-start(f32[64,1,128]{2,1,0:T(1,128)} %bitcast.3), calls=%async_computation.1 | async-start | bytes 65536 | tf_op jit(solution)/shard_map/all_to_all | solution.py:431
  20.0 5.5 %collective-permute-start = (f32[64,128]{1,0:T(8,128)}, f32[64,128]{1,0:T(8,128)S(1)}, u32[]{:S(2)}, u32[]{:S(2)}) collective-permute-start(f32[64,128]{1,0:T(8,128)} %get-tuple-element.14), channel_id=1, source_target_pairs={{0,1},{1,2},{2,3},{3,4},{4,5},{5,6},{6,7},{7,8},{8,9},{9,10},{10,1... | collective-permute-start | bytes 98312 | tf_op jit(solution)/shard_map/ppermute | solution.py:452
  23.6 5.4 %collective-permute-start.1 = (f32[64,128]{1,0:T(8,128)}, f32[64,128]{1,0:T(8,128)S(1)}, u32[]{:S(2)}, u32[]{:S(2)}) collective-permute-start(f32[64,128]{1,0:T(8,128)} %get-tuple-element.15), channel_id=1, source_target_pairs={{1,0},{2,1},{3,2},{4,3},{5,4},{6,5},{7,6},{8,7},{9,8},{10,9},{11,1... | collective-permute-start | bytes 98312 | tf_op jit(solution)/shard_map/ppermute | solution.py:453
  25.5 3.5 %copy-start.6 = (f32[64,128]{1,0:T(8,128)}, f32[64,128]{1,0:T(8,128)S(1)}, u32[]{:S(2)}) copy-start(f32[64,128]{1,0:T(8,128)S(1)} %collective-permute-done.low_ref) | copy-start | bytes 98308
  29.0 0.6 copy-start.7
  31.5 0.6 copy-start.2
  32.1 11.1 %all-to-all-start = ((f32[4,3,64,128]{3,2,1,0:T(8,128)}), f32[4,3,64,128]{3,2,1,0:T(8,128)S(1)}, u32[]{:S(2)}, u32[]{:S(2)}) async-start(f32[4,3,64,128]{3,2,1,0:T(8,128)} %spread.1), calls=%async_computation | async-start | bytes 786432 | tf_op jit(solution)/shard_map/all_to_all | solution.py:431
  39.7 3.4 %collective-permute-start.2 = (f32[4,8,128]{2,1,0:T(8,128)}, f32[4,8,128]{2,1,0:T(8,128)S(1)}, u32[]{:S(2)}, u32[]{:S(2)}) collective-permute-start(f32[4,8,128]{2,1,0:T(8,128)} %profile.1.own_ref), channel_id=1, source_target_pairs={{0,1},{1,2},{2,3},{3,4},{4,5},{5,6},{6,7},{7,8},{8,9},{9,10},{10,1... | collective-permute-start | bytes 49160 | tf_op jit(solution)/shard_map/ppermute | solution.py:486
  43.1 0.6 copy-start.9
  43.3 0.7 copy-start
  60.4 15.4 %copy-start.3 = (f32[64,1,128]{2,1,0:T(1,128)S(1)}, f32[64,1,128]{2,1,0:T(1,128)}, u32[]{:S(2)}) copy-start(f32[64,1,128]{2,1,0:T(1,128)} %copy-done.2) | copy-start | bytes 98308
  60.4 28.5 %all-to-all-start.3 = ((f32[64,8,128]{2,1,0:T(8,128)}), f32[64,8,128]{2,1,0:T(8,128)S(1)}, u32[]{:S(2)}, u32[]{:S(2)}) async-start(f32[64,8,128]{2,1,0:T(8,128)} %bitcast.20), calls=%async_computation.3 | async-start | bytes 524288 | tf_op jit(solution)/shard_map/all_to_all | solution.py:431
  88.9 0.7 copy-start.1
  112.3 4.6 %collective-permute-start.3 = (f32[64,128]{1,0:T(8,128)}, f32[64,128]{1,0:T(8,128)S(1)}, u32[]{:S(2)}, u32[]{:S(2)}) collective-permute-start(f32[64,128]{1,0:T(8,128)} %get-tuple-element.22), channel_id=1, source_target_pairs={{0,1},{1,2},{2,3},{3,4},{4,5},{5,6},{6,7},{7,8},{8,9},{9,10},{10,1... | collective-permute-start | bytes 98312 | tf_op jit(solution)/shard_map/ppermute | solution.py:523
  115.0 5.4 %collective-permute-start.4 = (f32[64,128]{1,0:T(8,128)}, f32[64,128]{1,0:T(8,128)S(1)}, u32[]{:S(2)}, u32[]{:S(2)}) collective-permute-start(f32[64,128]{1,0:T(8,128)} %get-tuple-element.23), channel_id=1, source_target_pairs={{1,0},{2,1},{3,2},{4,3},{5,4},{6,5},{7,6},{8,7},{9,8},{10,9},{11,1... | collective-permute-start | bytes 98312 | tf_op jit(solution)/shard_map/ppermute | solution.py:524
  116.9 3.5 %copy-start.4 = (f32[64,128]{1,0:T(8,128)}, f32[64,128]{1,0:T(8,128)S(1)}, u32[]{:S(2)}) copy-start(f32[64,128]{1,0:T(8,128)S(1)} %collective-permute-done.3.low_ref) | copy-start | bytes 98308
  120.4 0.6 copy-start.5
where the time goes:
time: 160 us; the launch traced here: 159 us
  blocking collectives  60.8 us (38%)
  starting transfers between devices  44.9 us (28%)
  Pallas kernels  22.8 us (14%)
  waiting for transfers between devices  20.5 us (13%)
  local copies, waits for them, and re-layouts  7.08 us (4%)
  other arithmetic  2.44 us (2%)
    all_to_all x4, blocking collectives, exchange(): return lax.all_to_all(array, axis, split_axis=0, concat_axis=0, tiled=True)  60.8 us
    all_to_all x3, starting transfers between devices, exchange(): return lax.all_to_all(array, axis, split_axis=0, concat_axis=0, tiled=True)  32.6 us
    all_to_all x3, waiting for transfers between devices, exchange(): return lax.all_to_all(array, axis, split_axis=0, concat_axis=0, tiled=True)  12.5 us
    ppermute x2, waiting for transfers between devices, on_device(): high = lax.ppermute(to_down, 'sub', down)  6.99 us
    ppermute x2, starting transfers between devices, on_device(): low = lax.ppermute(to_up, 'sub', up)  6.23 us
    unnamed x25, local copies, waits for them, and re-layouts  4.99 us
    pallas_call x1, Pallas kernels, on_device(): pl.pallas_call(forward_kernel, in_specs=[SM, VM, VM, VM], out_shape=(shap...  4 us
    ppermute x2, starting transfers between devices, on_device(): high = lax.ppermute(to_down, 'sub', down)  3.84 us
  transfers between devices with their start and end apart: 8, of which 5 were waited for; matrix products, arithmetic and copies ran while one was open for 0% of the time, Pallas kernels for 4%

commit v1 on v0

--- a/solution.py
+++ b/solution.py
@@ -71,40 +71,83 @@
     return low, high
 
 
-def edges_kernel(k_ref, f_ref, up_ref, down_ref):
-    kl, kh = edge_tile(k_ref[:, 384:512], k_ref[:, 0:128], HALO)
-    fl, fh = edge_tile(f_ref[:, 384:512], f_ref[:, 0:128], 3 * HALO)
-    up_ref[...] = kl + fl
-    down_ref[...] = kh + fh
-
-
-def spread_kernel(k_ref, f_ref, low_ref, high_ref, out_ref):
-    for q in range(4):
-        out_ref[q, 0] = k_ref[:, 128 * q : 128 * q + 128]
-        out_ref[q, 1] = f_ref[:, 128 * q : 128 * q + 128]
-        below = max(q - 1, 0)
-        above = min(q + 1, 3)
-        kl, kh = edge_tile(
-            k_ref[:, 128 * below : 128 * below + 128],
-            k_ref[:, 128 * above : 128 * above + 128],
-            HALO,
-        )
-        fl, fh = edge_tile(
-            f_ref[:, 128 * below : 128 * below + 128],
-            f_ref[:, 128 * above : 128 * above + 128],
-            3 * HALO,
-        )
-        low = low_ref[...] if q == 0 else kl + fl
-        high = high_ref[...] if q == 3 else kh + fh
-        out_ref[q, 2] = low + high
-
-
-def profile_kernel(step_ref, modes_ref, out_ref):
-    steps = step_ref[...]
-    total = jnp.zeros((64, 128), F32)
-    for j in range(8):
-        total = total + steps[:, j : j + 1] * modes_ref[pl.ds(j, 64, stride=8), :]
-    out_ref[0] = jnp.broadcast_to(jnp.sum(total, axis=0, keepdims=True), (8, 128))
+def prepare_kernel(
+    place_ref, k_ref, f_ref, owner_ref, row_ref, step_ref, *outs
+):
+    message_ref, slot_ref = outs[4:]
+    owner_row = owner_ref[...]
+    owner = jnp.transpose(jnp.broadcast_to(owner_row.astype(F32), (8, 256)))[:, 0:1]
+    row = jnp.transpose(jnp.broadcast_to(row_ref[...].astype(F32), (8, 256)))[:, 0:1]
+    same = owner == owner_row.astype(F32)
+    i, j = sub((256, 256)), lane((256, 256))
+    rank = jnp.sum(jnp.where(same & (j < i), 1.0, 0.0), axis=1, keepdims=True)
+    rank_row = jnp.sum(jnp.where(same & (i < j), 1.0, 0.0), axis=0, keepdims=True)
+    slots = owner_row * SLOTS + rank_row.astype(jnp.int32)
+    slot_ref[...] = slots
+    held = jnp.where(owner_row == sub((64, 256)), 1.0, 0.0).astype(BF)
+    n = lane((256, 128))
+    named = jnp.where(n == SLOTS + rank.astype(jnp.int32), row - float(VROWS), 0.0).astype(BF)
+    n, m = lane((64, 128)), sub((64, 128))
+    message = jnp.dot(held, named, preferred_element_type=F32) + jnp.where(
+        (n >= SLOTS) & (n < 2 * SLOTS), float(VROWS), 0.0
+    )
+    spots = jnp.broadcast_to(slots.astype(F32), (8, 256))
+    for q, towards in ((3, 1), (0, -1)):
+        chosen = jnp.where(sub((256, 128)) == 4 * (lane((256, 128)) - 64) + q, 1.0, 0.0)
+        told = select_dot(spots, chosen.astype(BF))[0:1]
+        message = jnp.where((m == place_ref[1] + towards) & (n >= 64), told, message)
+    message_ref[...] = message
+    message_ref[:, 0:8] = jnp.broadcast_to(step_ref[...], (64, 8))
+    for far in range(4):
+        q = (place_ref[0] + far) & 3
+        own = pl.ds(pl.multiple_of(128 * q, 128), 128)
+        below = pl.ds(pl.multiple_of(128 * jnp.maximum(q - 1, 0), 128), 128)
+        above = pl.ds(pl.multiple_of(128 * jnp.minimum(q + 1, 3), 128), 128)
+        outs[far][0] = k_ref[:, own]
+        outs[far][1] = f_ref[:, own]
+        halo = jnp.zeros((64, 128), F32)
+        for ref, shift in ((k_ref, HALO), (f_ref, 3 * HALO)):
+            low, high = edge_tile(ref[:, below], ref[:, above], shift)
+            halo = halo + jnp.where(q > 0, low, 0.0) + jnp.where(q < 3, high, 0.0)
+        outs[far][2] = halo
+
+
+def border_kernel(
+    place_ref, heard_ref, modes_ref, slab_0, slab_1, slab_2, slab_3,
+    profile_ref, slot_ref, out_ref, tile,
+):
+    q, u = place_ref[0], place_ref[1]
+    heard = heard_ref[...]
+    steps = [jnp.broadcast_to(heard[:, j : j + 1], (64, 128)) for j in range(8)]
+    for c in range(4):
+        tile[c] = modes_ref[:, 128 * c : 128 * c + 128]
+        total = jnp.zeros((64, 128), F32)
+        for j in range(8):
+            total = total + steps[j] * tile[c, pl.ds(j, 64, stride=8), :]
+        profile_ref[c] = jnp.broadcast_to(jnp.sum(total, axis=0, keepdims=True), (8, 128))
+    m = sub((64, 128))
+    for side, other in enumerate((u - 1, u + 1)):
+        told = jnp.sum(jnp.where(m == other, heard, 0.0), axis=0, keepdims=True)
+        slot_ref[side : side + 1] = pltpu.roll(told, 64, 1).astype(jnp.int32)
+    n = lane((64, 128))
+    sent = jnp.zeros((64, 128), F32)
+    for far, slab_ref in enumerate((slab_0, slab_1, slab_2, slab_3)):
+        k, f = slab_ref[0], slab_ref[1]
+        k = jnp.where(n < HALO, jnp.where(q == 3, pltpu.roll(k, HALO, 1), k), 0.0)
+        f = jnp.where(n < HALO, jnp.where(q == 3, pltpu.roll(f, HALO, 1), f), 0.0)
+        both = k + pltpu.roll(f, HALO, 1)
+        sent = sent + pltpu.roll(both, 2 * HALO * ((q - far) & 3), 1)
+    out_ref[0:64] = sent
+    out_ref[64:72] = jnp.where(q == 3, profile_ref[3], profile_ref[0])
+
+
+def halo_from(near, g, first):
+    n = lane((64, 128))
+    x = pltpu.roll(near, (128 - 2 * HALO * g) & 127, 1)
+    k = jnp.where(n < HALO, x, 0.0)
+    f = jnp.where((n >= HALO) & (n < 2 * HALO), x, 0.0)
+    low = k + pltpu.roll(f, HALO, 1)
+    return jnp.where(first, low, pltpu.roll(low, HALO, 1))
 
 
 def shifted(x, amount):
@@ -301,20 +344,27 @@
     fine.scan(2, relaxed, finish)
 
 
-def forward_kernel(place_ref, in_ref, own_ref, near_ref, out_ref, kf_ref, natural, *scratch):
+def forward_kernel(
+    place_ref, slab_0, slab_1, slab_2, slab_3, own_ref, near_ref, out_ref, kf_ref, natural, *scratch
+):
+    q = place_ref[0]
+    outer = near_ref[0:64]
+    chosen = [to_pairs_matrix(2 * HALO * field) for field in range(2)]
+    for far, slab_ref in enumerate((slab_0, slab_1, slab_2, slab_3)):
+        g = (q - far) & 3
+        halo = slab_ref[2] + halo_from(outer, g, q == 0)
+        rows = pl.ds(pl.multiple_of(64 * g, 64), 64)
+        for field in range(2):
+            x = jnp.concatenate([slab_ref[field], halo], axis=1)
+            got = select_dot(x, chosen[field])
+            natural[2 * field, rows, :] = got[:, :128]
+            natural[2 * field + 1, rows, :] = got[:, 128:]
     for field in range(2):
-        chosen = to_pairs_matrix(2 * HALO * field)
-        for g in range(4):
-            x = jnp.concatenate([in_ref[g, field], in_ref[g, 2]], axis=1)
-            got = select_dot(x, chosen)
-            natural[0, 64 * g : 64 * g + 64] = got[:, :128]
-            natural[1, 64 * g : 64 * g + 64] = got[:, 128:]
         for p in range(2):
             for t in range(T):
-                kf_ref[2 * field + p, t] = natural[p, pl.ds(t, 8, stride=T), :]
-    q = place_ref[0]
-    low = jnp.where(q == 0, near_ref[3], own_ref[jnp.maximum(q - 1, 0)])
-    high = jnp.where(q == 3, near_ref[0], own_ref[jnp.minimum(q + 1, 3)])
+                kf_ref[2 * field + p, t] = natural[2 * field + p, pl.ds(t, 8, stride=T), :]
+    low = jnp.where(q == 0, near_ref[64:72], own_ref[jnp.maximum(q - 1, 0)])
+    high = jnp.where(q == 3, near_ref[64:72], own_ref[jnp.minimum(q + 1, 3)])
     parts = edge_tile(low, high, HALO)
     profile = select_dot(
         jnp.concatenate([own_ref[q], parts[0] + parts[1]], axis=1), to_pairs_matrix(0)
@@ -345,17 +395,23 @@
         field_ref[:, 128 * q : 128 * q + 128] = in_ref[q]
     out_ref[...] = jnp.zeros(out_ref.shape, F32)
     for i in range(256):
-        out_ref[pl.ds(slot_ref[i], 1), :] = in_ref[i // 64, i % 64 : i % 64 + 1]
-
-
-def voxel_kernel(in_ref, row_ref, weight_ref, spread_ref, response_ref, out_ref):
-    rows = jnp.broadcast_to(row_ref[...], (VROWS, 512))
+        r, q = divmod(i, 4)
+        out_ref[pl.ds(slot_ref[i], 1), :] = in_ref[q, r : r + 1]
+
+
+def voxel_kernel(in_ref, heard_ref, weight_ref, spread_ref, response_ref, out_ref):
+    p = lane((128, 512))
+    spot = jnp.where(sub((128, 512)) == SLOTS + (p & (SLOTS - 1)), 1.0, 0.0).astype(BF)
+    rows = jnp.dot(heard_ref[...].astype(BF), spot, preferred_element_type=F32)
+    mine = (lane((64, 512)) >> 3) == sub((64, 512))
+    rows = jnp.sum(jnp.where(mine, rows, 0.0), axis=0, keepdims=True)
+    rows = jnp.broadcast_to(rows, (VROWS, 512))
     mask = jnp.where(rows == sub((VROWS, 512)).astype(F32), 1.0, 0.0)
-    hi, mid, lo = split3(in_ref[...])
     chosen = mask.astype(BF)
-    voxels = jnp.dot(chosen, lo, preferred_element_type=F32)
-    voxels = voxels + jnp.dot(chosen, mid, preferred_element_type=F32)
-    voxels = voxels + jnp.dot(chosen, hi, preferred_element_type=F32)
+    voxels = None
+    for part in reversed(split3(in_ref[...])):
+        got = jnp.dot(chosen, part, preferred_element_type=F32)
+        voxels = got if voxels is None else voxels + got
     spread = spread_ref[...]
     response = lax.dot_general(
         voxels, spread, (((1,), (1,)), ((), ())), precision=HIGH, preferred_element_type=F32
@@ -369,29 +425,47 @@
     for part in reversed(split3(weighted)):
         got = jnp.dot(back, part, preferred_element_type=F32)
         total = got if total is None else total + got
-    out_ref[...] = total
-
-
-def unpack_kernel(slot_ref, in_ref, out_ref, up_ref, down_ref):
+    n = lane((8, 128))
+    width = SLOTS + 2
+    blank = jnp.zeros((1, 128), F32)
+    out_ref[SLOTS] = blank
+    out_ref[width * 63 + SLOTS + 1] = blank
+    for u in range(64):
+        own = total[SLOTS * u : SLOTS * u + SLOTS]
+        for k in range(SLOTS):
+            out_ref[width * u + k] = own[k : k + 1]
+        if u < 63:
+            last = jnp.where(n < HALO, pltpu.roll(own, HALO, 1), 0.0)
+            last = pltpu.roll(last, 0, 1, stride=16, stride_axis=0)
+            out_ref[width * (u + 1) + SLOTS] = jnp.sum(last, axis=0, keepdims=True)
+        if u > 0:
+            first = jnp.where(n < HALO, own, 0.0)
+            first = pltpu.roll(first, 0, 1, stride=16, stride_axis=0)
+            out_ref[width * (u - 1) + SLOTS + 1] = jnp.sum(first, axis=0, keepdims=True)
+
+
+def driving_kernel(slot_ref, near_ref, in_ref, out_ref, ends):
     for i in range(256):
-        out_ref[i // 64, i % 64 : i % 64 + 1] = in_ref[pl.ds(slot_ref[i], 1), :]
-    low, high = edge_tile(out_ref[3], out_ref[0], HALO)
-    up_ref[...] = low
-    down_ref[...] = high
-
-
-def driving_kernel(in_ref, low_ref, high_ref, out_ref):
+        r, q = divmod(i, 4)
+        at = slot_ref[i]
+        out_ref[q, 0, r : r + 1] = in_ref[at + 2 * (at >> 3)]
+    for side in range(2):
+        for r in range(64):
+            at = near_ref[side, r]
+            row = in_ref[(SLOTS + 2) * (at >> 3) + SLOTS + side]
+            turn = (128 - 16 * (at & 7) + HALO * side) & 127
+            ends[side, r : r + 1] = pltpu.roll(row, turn, 1)
+    n = lane((64, 128))
     for q in range(4):
-        out_ref[q, 0] = in_ref[q]
-        low, high = edge_tile(in_ref[max(q - 1, 0)], in_ref[min(q + 1, 3)], HALO)
+        low, high = edge_tile(out_ref[max(q - 1, 0), 0], out_ref[min(q + 1, 3), 0], HALO)
         if q == 0:
-            low = low_ref[...]
+            low = jnp.where(n < HALO, ends[0], 0.0)
         if q == 3:
-            high = high_ref[...]
+            high = jnp.where((n >= HALO) & (n < 2 * HALO), ends[1], 0.0)
         out_ref[q, 1] = low + high
 
 
-def adjoint_kernel(place_ref, in_ref, kf_ref, modes_ref, out_ref, natural, begin, *scratch):
+def adjoint_kernel(place_ref, in_ref, kf_ref, modes_ref, out_ref, tile, natural, begin, *scratch):
     chosen = to_pairs_matrix(0)
     for g in range(4):
         x = jnp.concatenate([in_ref[g, 0], in_ref[g, 1]], axis=1)
@@ -413,18 +487,46 @@
     natural_flux = select_dot(jnp.concatenate(flux, axis=1), from_pairs_matrix())
     row = natural_flux[0:1]
     out = jnp.zeros((256, 128), F32)
+    column = pl.multiple_of(place_ref[0] * 128, 128)
+    tile[...] = modes_ref[:, pl.ds(column, 128)]
     for j in range(2):
-        part = jnp.sum(modes_ref[pl.ds(j, 256, stride=2), :] * row, axis=1, keepdims=True)
+        modes = tile[pl.ds(j, 256, stride=2), :]
+        part = jnp.sum(modes * row, axis=1, keepdims=True)
         out = jnp.where(lane((256, 128)) == j, part, out)
     out_ref[...] = out
 
 
 VM = pl.BlockSpec(memory_space=pltpu.VMEM)
 SM = pl.BlockSpec(memory_space=pltpu.SMEM)
-
-
-def shape(*dims):
-    return jax.ShapeDtypeStruct(dims, F32)
+PARAMS = pltpu.CompilerParams(vmem_limit_bytes=16 << 20)
+
+
+def near(array):
+    return pltpu.with_memory_space_constraint(array, pltpu.VMEM)
+
+
+def held(*dims, dtype=F32):
+    return pltpu.VMEM(dims, dtype)
+
+
+def run(kernel, name, ins, outs, scratch=(), pinned=True):
+    scalars = [array.dtype == jnp.int32 and name != "prepare" for array in ins]
+    scalars[0] = ins[0].dtype == jnp.int32
+    specs = [SM if scalar else VM if pinned else pl.BlockSpec() for scalar in scalars]
+    if pinned:
+        ins = [array if scalar else near(array) for array, scalar in zip(ins, scalars)]
+    else:
+        ins = [array if scalar else pltpu.with_memory_space_constraint(array, pltpu.HBM)
+               for array, scalar in zip(ins, scalars)]
+    return pl.pallas_call(
+        kernel,
+        in_specs=specs,
+        out_specs=[VM] * len(outs),
+        out_shape=outs,
+        scratch_shapes=list(scratch),
+        compiler_params=PARAMS,
+        name=name,
+    )(*ins)
 
 
 def exchange(array, axis):
@@ -442,111 +544,81 @@
     spread_matrix,
 ):
     count = lax.axis_size("sub")
-    place = lax.axis_index("seg").astype(jnp.int32).reshape(1)
-    up = [(i, i + 1) for i in range(count - 1)]
-    down = [(i + 1, i) for i in range(count - 1)]
-
-    to_up, to_down = pl.pallas_call(
-        edges_kernel, out_shape=(shape(64, 128), shape(64, 128)), name="edges"
-    )(diffusivity, background_flow)
-    low = lax.ppermute(to_up, "sub", up)
-    high = lax.ppermute(to_down, "sub", down)
-
-    owners = brick_owner.reshape(64, 4).T.reshape(256)
-    rows = voxel_row.reshape(64, 4).T.reshape(256)
-    index = jnp.arange(256, dtype=jnp.int32)
-    earlier = (owners[:, None] == owners[None, :]) & (index[:, None] < index[None, :])
-    slots = owners * SLOTS + jnp.sum(earlier.astype(jnp.int32), axis=0)
-    named = slots[:, None] == jnp.arange(count * SLOTS, dtype=jnp.int32)[None, :]
-    slot_rows = VROWS - jnp.sum(jnp.where(named, VROWS - rows[:, None], 0), axis=0)
-    message = jnp.concatenate(
+    place = jnp.stack([lax.axis_index("seg"), lax.axis_index("sub")]).astype(jnp.int32)
+
+    *slab, message, slots = run(
+        prepare_kernel,
+        "prepare",
+        (
+            place,
+            diffusivity,
+            background_flow,
+            brick_owner.reshape(1, 256),
+            voxel_row.reshape(1, 256),
+            profile_step.reshape(1, 8),
+        ),
+        (held(3, 64, 128),) * 4 + (held(64, 128), held(1, 256, dtype=jnp.int32)),
+        pinned=False,
+    )
+    slots = slots.reshape(256)
+    for far in (2, 1, 3):
+        slab[far] = lax.ppermute(slab[far], "seg", [(i, (i + far) % 4) for i in range(4)])
+    heard = exchange(message.reshape(count, 1, 128), "sub").reshape(count, 128)
+
+    own_profile, near_slots, to_near = run(
+        border_kernel,
+        "border",
+        (place, heard, inlet_modes, *slab),
+        (held(4, 8, 128), held(2, 128, dtype=jnp.int32), held(72, 128)),
+        [pltpu.VMEM((4, 512, 128), F32)],
+    )
+    outward = [(3 * count + i, i + 1) for i in range(count - 1)]
+    outward += [(i + 1, 3 * count + i) for i in range(count - 1)]
+    from_near = lax.ppermute(to_near, ALL, outward)
+
+    field, kf = run(
+        forward_kernel,
+        "forward",
+        (place, *slab, own_profile, from_near),
+        (held(256, 128), held(4, T, 8, 128)),
+        [pltpu.VMEM((4, 256, 128), F32)] + SOLVE_SCRATCH,
+    )
+    back = exchange(field.reshape(4, 64, 128), "seg")
+
+    forward_field, packed = run(
+        pack_kernel, "pack", (slots, back), (held(64, 512), held(count * SLOTS, 128))
+    )
+    arrived = exchange(packed.reshape(count, SLOTS, 128), "sub")
+
+    response, answer = run(
+        voxel_kernel,
+        "voxels",
+        (arrived.reshape(count * SLOTS, 128), heard, noise_weight, spread_matrix),
+        (held(VROWS, 128), held(count * (SLOTS + 2), 1, 128)),
+    )
+    answered = exchange(answer, "sub")
+
+    (spread,) = run(
+        driving_kernel,
+        "driving",
+        (slots, near_slots, answered),
+        (held(4, 2, 64, 128),),
+        [pltpu.VMEM((2, 64, 128), F32)],
+    )
+    slab = exchange(spread, "seg")
+
+    (partial,) = run(
+        adjoint_kernel,
+        "adjoint",
+        (place, slab, kf, inlet_modes),
+        (held(256, 128),),
         [
-            jnp.broadcast_to(profile_step[None, :], (count, 8)),
-            slot_rows.reshape(count, SLOTS).astype(F32),
-            jnp.zeros((count, 112), F32),
-        ],
-        axis=1,
-    )
-    heard = exchange(message.reshape(count, 1, 128), "sub").reshape(count, 128)
-    heard_rows = heard[:, 8:16].reshape(1, count * SLOTS)
-
-    own_profile = pl.pallas_call(
-        profile_kernel,
-        grid=(4,),
-        in_specs=[
-            pl.BlockSpec((64, 128), lambda c: (0, 0)),
-            pl.BlockSpec((512, 128), lambda c: (0, c)),
-        ],
-        out_specs=pl.BlockSpec((1, 8, 128), lambda c: (c, 0, 0)),
-        out_shape=shape(4, 8, 128),
-        name="profile",
-    )(heard, inlet_modes)
-    ends = [(i, i + 1) for i in range(count - 1)]
-    ends += [(3 * count + i + 1, 3 * count + i) for i in range(count - 1)]
-    near_profile = lax.ppermute(own_profile, ALL, ends)
-
-    spread = pl.pallas_call(
-        spread_kernel, out_shape=shape(4, 3, 64, 128), name="spread"
-    )(diffusivity, background_flow, low, high)
-    slab = exchange(spread, "seg")
-
-    field, kf = pl.pallas_call(
-        forward_kernel,
-        in_specs=[SM, VM, VM, VM],
-        out_shape=(shape(256, 128), shape(4, T, 8, 128)),
-        scratch_shapes=[pltpu.VMEM((2, 256, 128), F32)] + SOLVE_SCRATCH,
-        name="forward",
-    )(place, slab, own_profile, near_profile)
-    back = exchange(field.reshape(4, 64, 128), "seg")
-
-    forward_field, packed = pl.pallas_call(
-        pack_kernel,
-        in_specs=[SM, VM],
-        out_shape=(shape(64, 512), shape(count * SLOTS, 128)),
-        name="pack",
-    )(slots, back)
-    arrived = exchange(packed.reshape(count, SLOTS, 128), "sub")
-
-    response, answer = pl.pallas_call(
-        voxel_kernel,
-        out_shape=(shape(VROWS, 128), shape(count * SLOTS, 128)),
-        name="voxels",
-    )(arrived.reshape(count * SLOTS, 128), heard_rows, noise_weight, spread_matrix)
-    answered = exchange(answer.reshape(count, SLOTS, 128), "sub")
-
-    driving, to_up, to_down = pl.pallas_call(
-        unpack_kernel,
-        in_specs=[SM, VM],
-        out_shape=(shape(4, 64, 128), shape(64, 128), shape(64, 128)),
-        name="unpack",
-    )(slots, answered.reshape(count * SLOTS, 128))
-    low = lax.ppermute(to_up, "sub", up)
-    high = lax.ppermute(to_down, "sub", down)
-    spread = pl.pallas_call(
-        driving_kernel, out_shape=shape(4, 2, 64, 128), name="driving"
-    )(driving, low, high)
-    slab = exchange(spread, "seg")
-
-    partial = pl.pallas_call(
-        adjoint_kernel,
-        grid_spec=pltpu.PrefetchScalarGridSpec(
-            num_scalar_prefetch=1,
-            grid=(1,),
-            in_specs=[
-                pl.BlockSpec((4, 2, 64, 128), lambda i, q: (0, 0, 0, 0)),
-                pl.BlockSpec((4, T, 8, 128), lambda i, q: (0, 0, 0, 0)),
-                pl.BlockSpec((512, 128), lambda i, q: (0, q[0])),
-            ],
-            out_specs=pl.BlockSpec((256, 128), lambda i, q: (0, 0)),
-            scratch_shapes=[
-                pltpu.VMEM((2, 256, 128), F32),
-                pltpu.VMEM((2, T, 8, 128), F32),
-            ]
-            + SOLVE_SCRATCH,
-        ),
-        out_shape=shape(256, 128),
-        name="adjoint",
-    )(place, slab, kf, inlet_modes)
+            pltpu.VMEM((512, 128), F32),
+            pltpu.VMEM((2, 256, 128), F32),
+            pltpu.VMEM((2, T, 8, 128), F32),
+        ]
+        + SOLVE_SCRATCH,
+    )
     gathered = exchange(partial.reshape(256, 1, 128), ALL)
     product = jnp.sum(gathered, axis=(0, 1))[:2]
     return (forward_field, response, product)

time: 160 us -> 126 us (0.79)
  starting transfers between devices: 44.9 us -> 14.4 us
  blocking collectives: 60.8 us -> 78.7 us
  Pallas kernels: 22.8 us -> 12.3 us
  waiting for transfers between devices: 20.5 us -> 15.9 us
  local copies, waits for them, and re-layouts: 7.08 us -> 2.49 us
    all_to_all x3 -> x1, starting transfers between devices: 32.6 us -> 6.28 us  [exchange(): return lax.all_to_all(array, axis, split_axis=0, concat_axis=0, tiled=True)]
    all_to_all x4 -> x5, blocking collectives: 60.8 us -> 78.7 us  [exchange(): return lax.all_to_all(array, axis, split_axis=0, concat_axis=0, tiled=True)]
    pallas_call x9 -> x7, Pallas kernels: 22.8 us -> 12.3 us  [run(): pl.pallas_call(kernel, in_specs=specs, out_specs=[VM] * len(outs), out_sh...]
    ppermute x5 -> x4, starting transfers between devices: 12.4 us -> 8.07 us  [the longest x3 5.88 us: on_device(): lax.ppermute(slab[far], 'seg', [(i, (i + far) % 4) for i in range(4)])]
    ppermute x5 -> x4, waiting for transfers between devices: 8.05 us -> 4.29 us  [the longest x1 4.28 us: on_device(): from_near = lax.ppermute(to_near, ALL, outward)]
    unnamed x25 -> x10, local copies, waits for them, and re-layouts: 4.99 us -> 2.49 us
    all_to_all x3 -> x1, waiting for transfers between devices: 12.5 us -> 11.6 us  [exchange(): return lax.all_to_all(array, axis, split_axis=0, concat_axis=0, tiled=True)]
  transfers between devices with their start and end apart: 8 -> 5, of which waited for: 5 -> 2; matrix products, arithmetic and copies ran while one was open for 0% -> 1% of each run, Pallas kernels for 4% -> 0%
where the time goes in v1:
time: 126 us; the launch traced here: 125 us
  blocking collectives  78.7 us (62%)
  waiting for transfers between devices  15.9 us (13%)
  starting transfers between devices  14.4 us (11%)
  Pallas kernels  12.3 us (10%)
  local copies, waits for them, and re-layouts  2.49 us (2%)
    all_to_all x5, blocking collectives, exchange(): return lax.all_to_all(array, axis, split_axis=0, concat_axis=0, tiled=True)  78.7 us
    pallas_call x7, Pallas kernels, run(): pl.pallas_call(kernel, in_specs=specs, out_specs=[VM] * len(outs), out_sh...  12.3 us
    all_to_all x1, waiting for transfers between devices, exchange(): return lax.all_to_all(array, axis, split_axis=0, concat_axis=0, tiled=True)  11.6 us
    all_to_all x1, starting transfers between devices, exchange(): return lax.all_to_all(array, axis, split_axis=0, concat_axis=0, tiled=True)  6.28 us
    ppermute x3, starting transfers between devices, on_device(): lax.ppermute(slab[far], 'seg', [(i, (i + far) % 4) for i in range(4)])  5.88 us
    ppermute x1, waiting for transfers between devices, on_device(): from_near = lax.ppermute(to_near, ALL, outward)  4.28 us
  transfers between devices with their start and end apart: 5, of which 2 were waited for; matrix products, arithmetic and copies ran while one was open for 1% of the time, Pallas kernels for 0%

profile of v1, /device:TPU:1, one launch (start us, length us, event | category | flops | bytes accessed | tf_op | source)
XLA Modules:
  0.0 125.3 jit_solution(6190271954345099769)
XLA Ops:
  0.6 0.1 pad_add_fusion.place_ref
  0.7 1.5 %prepare.1 = (f32[3,64,128]{2,1,0:T(8,128)S(1)}, f32[3,64,128]{2,1,0:T(8,128)S(1)}, f32[3,64,128]{2,1,0:T(8,128)S(1)}, f32[3,64,128]{2,1,0:T(8,128)S(1)}, f32[64,128]{1,0:T(8,128)S(1)}, /*index=5*/s32[1,256]{1,0:T(1,128)S(1)}) custom-call(s32[2]{0:T(128)S(1)} %pad_add_fusion.place_ref, f32[64,512]{1,0:T(8,128)} %k_ref.1, f32[64,512]{1,0:T(8,128)} %f_ref.1, ...), custom_call_target="tpu_custom_call" | custom-call | tf_op jit(solution)/shard_map/prepare/pallas_call | solution.py:521
  2.2 2.2 %collective-permute-start = (f32[3,64,128]{2,1,0:T(8,128)S(1)}, f32[3,64,128]{2,1,0:T(8,128)S(1)}, u32[]{:S(2)}, u32[]{:S(2)}) collective-permute-start(f32[3,64,128]{2,1,0:T(8,128)S(1)} %get-tuple-element.20), channel_id=1, source_target_pairs={{0,64},{64,128},{128,192},{192,0},{1,65},{65,129},{129,193},{193,1... | collective-permute-start | bytes 294920 | tf_op jit(solution)/shard_map/ppermute | solution.py:565
  4.4 2.6 %collective-permute-start.1 = (f32[3,64,128]{2,1,0:T(8,128)S(1)}, f32[3,64,128]{2,1,0:T(8,128)S(1)}, u32[]{:S(2)}, u32[]{:S(2)}) collective-permute-start(f32[3,64,128]{2,1,0:T(8,128)S(1)} %get-tuple-element.21), channel_id=1, source_target_pairs={{0,128},{64,192},{128,0},{192,64},{1,129},{65,193},{129,1},{193,65... | collective-permute-start | bytes 294920 | tf_op jit(solution)/shard_map/ppermute | solution.py:565
  7.0 1.1 collective-permute-start.2
  8.1 22.2 %all_to_all.30 = f32[64,1,128]{2,1,0:T(1,128)S(1)} all-to-all(f32[64,1,128]{2,1,0:T(1,128)S(1)} %bitcast.22), channel_id=1, replica_groups=mesh['seg'=4,'sub'=64] {'sub'}, dimensions={0} | all-to-all | bytes 65536 | tf_op jit(solution)/shard_map/all_to_all | solution.py:533
  30.3 0.0 collective-permute-done.slab_1
  30.3 0.0 collective-permute-done.1.slab_2
  30.3 0.0 collective-permute-done.2.slab_3
  30.3 0.0 copy-start
  30.3 1.2 copy-done
  31.5 1.1 border.1
  32.6 2.2 %collective-permute-start.3 = (f32[72,128]{1,0:T(8,128)S(1)}, f32[72,128]{1,0:T(8,128)S(1)}, u32[]{:S(2)}, u32[]{:S(2)}) collective-permute-start(f32[72,128]{1,0:T(8,128)S(1)} %get-tuple-element.25), channel_id=1, source_target_pairs={{192,1},{193,2},{194,3},{195,4},{196,5},{197,6},{198,7},{199,8},{2... | collective-permute-start | bytes 110600 | tf_op jit(solution)/shard_map/ppermute | solution.py:577
  34.8 4.3 %collective-permute-done.3.near_ref = f32[72,128]{1,0:T(8,128)S(1)} collective-permute-done((f32[72,128]{1,0:T(8,128)S(1)}, f32[72,128]{1,0:T(8,128)S(1)}, u32[]{:S(2)}, u32[]{:S(2)}) %collective-permute-start.3) | collective-permute-done | bytes 36896 | tf_op jit(solution)/shard_map/ppermute | solution.py:577
  39.1 3.3 %forward.1 = (f32[256,128]{1,0:T(8,128)S(1)}, f32[4,32,8,128]{3,2,1,0:T(8,128)S(1)}) custom-call(s32[2]{0:T(128)S(1)} %pad_add_fusion.place_ref, f32[3,64,128]{2,1,0:T(8,128)S(1)} %get-tuple-element.19.slab_0, f32[3,64,128]{2,1,0:T(8,128)S(1)} %collective-permute-done.slab_1, f32[3,64,128]{2,1,0:T(8,128)S(1)} %collective-permute-done.1.slab_2, ...), custom_call_target="tpu_custom_call" | custom-call | tf_op jit(solution)/shard_map/forward/pallas_call | solution.py:521
  42.4 7.9 %all_to_all.31.in_ref = f32[4,64,128]{2,1,0:T(8,128)S(1)} all-to-all(f32[4,64,128]{2,1,0:T(8,128)S(1)} %bitcast.21), channel_id=1, replica_groups=mesh['seg'=4,'sub'=64] {'seg'}, dimensions={0} | all-to-all | bytes 262144 | tf_op jit(solution)/shard_map/all_to_all | solution.py:533
  50.3 0.7 pack.1
  51.0 0.0 copy-start.2
  51.0 0.0 copy-start.3
  51.0 21.0 %all_to_all.32 = f32[64,8,128]{2,1,0:T(8,128)S(1)} all-to-all(f32[64,8,128]{2,1,0:T(8,128)S(1)} %bitcast.20), channel_id=1, replica_groups=mesh['seg'=4,'sub'=64] {'sub'}, dimensions={0} | all-to-all | bytes 524288 | tf_op jit(solution)/shard_map/all_to_all | solution.py:533
  72.0 0.0 copy-done.2
  72.0 0.0 copy-done.3
  72.0 0.0 copy-start.1
  72.0 1.3 %voxels.1 = (f32[16,128]{1,0:T(8,128)S(1)}, f32[640,1,128]{2,1,0:T(1,128)S(1)}) custom-call(f32[512,128]{1,0:T(8,128)S(1)} %bitcast.17, f32[64,128]{1,0:T(8,128)S(1)} %bitcast.19, f32[16,128]{1,0:T(8,128)S(1)} %copy-done.3, f32[128,128]{1,0:T(8,128)S(1)} %copy-done.2), custom_call_target="tpu_custom_call" | custom-call | tf_op jit(solution)/shard_map/voxels/pallas_call | solution.py:521
  73.3 18.8 %all_to_all.33.in_ref = f32[640,1,128]{2,1,0:T(1,128)S(1)} all-to-all(f32[640,1,128]{2,1,0:T(1,128)S(1)} %get-tuple-element.31), channel_id=1, replica_groups=mesh['seg'=4,'sub'=64] {'sub'}, dimensions={0} | all-to-all | bytes 655360 | tf_op jit(solution)/shard_map/all_to_all | solution.py:533
  92.1 1.3 %driving.1 = f32[4,2,64,128]{3,2,1,0:T(8,128)S(1)} custom-call(s32[256]{0:T(256)S(1)} %bitcast.24, s32[2,128]{1,0:T(2,128)S(1)} %get-tuple-element.30.near_ref, f32[640,1,128]{2,1,0:T(1,128)S(1)} %all_to_all.33.in_ref), custom_call_target="tpu_custom_call" | custom-call | tf_op jit(solution)/shard_map/driving/pallas_call | solution.py:521
  93.4 8.8 %all_to_all.34.in_ref = f32[4,2,64,128]{3,2,1,0:T(8,128)S(1)} all-to-all(f32[4,2,64,128]{3,2,1,0:T(8,128)S(1)} %driving.1), channel_id=1, replica_groups=mesh['seg'=4,'sub'=64] {'seg'}, dimensions={0} | all-to-all | bytes 524288 | tf_op jit(solution)/shard_map/all_to_all | solution.py:533
  102.2 0.0 copy-done.1
  102.2 3.2 %adjoint.1 = f32[256,128]{1,0:T(8,128)} custom-call(s32[2]{0:T(128)S(1)} %pad_add_fusion.place_ref, f32[4,2,64,128]{3,2,1,0:T(8,128)S(1)} %all_to_all.34.in_ref, f32[4,32,8,128]{3,2,1,0:T(8,128)S(1)} %get-tuple-element.32.kf_ref, f32[512,512]{1,0:T(8,128)S(1)} %copy-done.1), custom_call_target="tpu_custom_call" | custom-call | tf_op jit(solution)/shard_map/adjoint/pallas_call | solution.py:521
  105.4 6.3 %all-to-all-start.5 = ((f32[256,1,128]{2,1,0:T(1,128)}), f32[256,1,128]{2,1,0:T(1,128)S(1)}, u32[]{:S(2)}, u32[]{:S(2)}) async-start(f32[256,1,128]{2,1,0:T(1,128)} %bitcast.13), calls=%async_computation.5 | async-start | bytes 262144 | tf_op jit(solution)/shard_map/all_to_all | solution.py:533
  111.7 0.7 copy.13
  112.3 0.6 copy.14
  112.9 11.6 %all-to-all-done.5 = f32[256,1,128]{2,1,0:T(1,128)S(1)} async-done(((f32[256,1,128]{2,1,0:T(1,128)}), f32[256,1,128]{2,1,0:T(1,128)S(1)}, u32[]{:S(2)}, u32[]{:S(2)}) %all-to-all-start.5) | async-done | bytes 131104 | tf_op jit(solution)/shard_map/all_to_all | solution.py:533
  124.5 0.8 reduce_sum.9
Async XLA Ops:
  2.2 28.1 %collective-permute-start = (f32[3,64,128]{2,1,0:T(8,128)S(1)}, f32[3,64,128]{2,1,0:T(8,128)S(1)}, u32[]{:S(2)}, u32[]{:S(2)}) collective-permute-start(f32[3,64,128]{2,1,0:T(8,128)S(1)} %get-tuple-element.20), channel_id=1, source_target_pairs={{0,64},{64,128},{128,192},{192,0},{1,65},{65,129},{129,193},{193,1... | collective-permute-start | bytes 294920 | tf_op jit(solution)/shard_map/ppermute | solution.py:565
  4.4 25.9 %collective-permute-start.1 = (f32[3,64,128]{2,1,0:T(8,128)S(1)}, f32[3,64,128]{2,1,0:T(8,128)S(1)}, u32[]{:S(2)}, u32[]{:S(2)}) collective-permute-start(f32[3,64,128]{2,1,0:T(8,128)S(1)} %get-tuple-element.21), channel_id=1, source_target_pairs={{0,128},{64,192},{128,0},{192,64},{1,129},{65,193},{129,1},{193,65... | collective-permute-start | bytes 294920 | tf_op jit(solution)/shard_map/ppermute | solution.py:565
  7.0 23.3 %collective-permute-start.2 = (f32[3,64,128]{2,1,0:T(8,128)S(1)}, f32[3,64,128]{2,1,0:T(8,128)S(1)}, u32[]{:S(2)}, u32[]{:S(2)}) collective-permute-start(f32[3,64,128]{2,1,0:T(8,128)S(1)} %get-tuple-element.22), channel_id=1, source_target_pairs={{0,192},{64,0},{128,64},{192,128},{1,193},{65,1},{129,65},{193,129... | collective-permute-start | bytes 294920 | tf_op jit(solution)/shard_map/ppermute | solution.py:565
  30.3 1.2 copy-start
  32.6 6.5 %collective-permute-start.3 = (f32[72,128]{1,0:T(8,128)S(1)}, f32[72,128]{1,0:T(8,128)S(1)}, u32[]{:S(2)}, u32[]{:S(2)}) collective-permute-start(f32[72,128]{1,0:T(8,128)S(1)} %get-tuple-element.25), channel_id=1, source_target_pairs={{192,1},{193,2},{194,3},{195,4},{196,5},{197,6},{198,7},{199,8},{2... | collective-permute-start | bytes 110600 | tf_op jit(solution)/shard_map/ppermute | solution.py:577
  51.0 21.0 %copy-start.2 = (f32[128,128]{1,0:T(8,128)S(1)}, f32[128,128]{1,0:T(8,128)}, u32[]{:S(2)}) copy-start(f32[128,128]{1,0:T(8,128)} %spread_ref.1) | copy-start | bytes 196612
  51.0 21.0 %copy-start.3 = (f32[16,128]{1,0:T(8,128)S(1)}, f32[16,128]{1,0:T(8,128)}, u32[]{:S(2)}) copy-start(f32[16,128]{1,0:T(8,128)} %weight_ref.1) | copy-start | bytes 24580
  72.0 30.2 %copy-start.1 = (f32[512,512]{1,0:T(8,128)S(1)}, f32[512,512]{1,0:T(8,128)}, u32[]{:S(2)}) copy-start(f32[512,512]{1,0:T(8,128)} %modes_ref.3) | copy-start | bytes 3145732
  105.4 19.1 %all-to-all-start.5 = ((f32[256,1,128]{2,1,0:T(1,128)}), f32[256,1,128]{2,1,0:T(1,128)S(1)}, u32[]{:S(2)}, u32[]{:S(2)}) async-start(f32[256,1,128]{2,1,0:T(1,128)} %bitcast.13), calls=%async_computation.5 | async-start | bytes 262144 | tf_op jit(solution)/shard_map/all_to_all | solution.py:533

commit v2 on v1

--- a/solution.py
+++ b/solution.py
@@ -72,9 +72,18 @@
 
 
 def prepare_kernel(
-    place_ref, k_ref, f_ref, owner_ref, row_ref, step_ref, *outs
+    place_ref, k_ref, f_ref, owner_ref, row_ref, step_ref, modes_ref, *outs
 ):
-    message_ref, slot_ref = outs[4:]
+    message_ref, slot_ref, tile, sems = outs[4:]
+    copies = []
+    for i in range(3):
+        start = 128 * jnp.clip(place_ref[0] + i - 1, 0, 3)
+        copies.append(
+            pltpu.make_async_copy(
+                modes_ref.at[:, pl.ds(pl.multiple_of(start, 128), 128)], tile.at[i], sems.at[i]
+            )
+        )
+        copies[-1].start()
     owner_row = owner_ref[...]
     owner = jnp.transpose(jnp.broadcast_to(owner_row.astype(F32), (8, 256)))[:, 0:1]
     row = jnp.transpose(jnp.broadcast_to(row_ref[...].astype(F32), (8, 256)))[:, 0:1]
@@ -110,25 +119,15 @@
             low, high = edge_tile(ref[:, below], ref[:, above], shift)
             halo = halo + jnp.where(q > 0, low, 0.0) + jnp.where(q < 3, high, 0.0)
         outs[far][2] = halo
+    for copy in copies:
+        copy.wait()
 
 
 def border_kernel(
-    place_ref, heard_ref, modes_ref, slab_0, slab_1, slab_2, slab_3,
-    profile_ref, slot_ref, out_ref, tile,
+    place_ref, tile, message_ref, slab_0, slab_1, slab_2, slab_3, out_ref, told_ref
 ):
-    q, u = place_ref[0], place_ref[1]
-    heard = heard_ref[...]
-    steps = [jnp.broadcast_to(heard[:, j : j + 1], (64, 128)) for j in range(8)]
-    for c in range(4):
-        tile[c] = modes_ref[:, 128 * c : 128 * c + 128]
-        total = jnp.zeros((64, 128), F32)
-        for j in range(8):
-            total = total + steps[j] * tile[c, pl.ds(j, 64, stride=8), :]
-        profile_ref[c] = jnp.broadcast_to(jnp.sum(total, axis=0, keepdims=True), (8, 128))
-    m = sub((64, 128))
-    for side, other in enumerate((u - 1, u + 1)):
-        told = jnp.sum(jnp.where(m == other, heard, 0.0), axis=0, keepdims=True)
-        slot_ref[side : side + 1] = pltpu.roll(told, 64, 1).astype(jnp.int32)
+    q = place_ref[0]
+    told_ref[...] = message_ref[...]
     n = lane((64, 128))
     sent = jnp.zeros((64, 128), F32)
     for far, slab_ref in enumerate((slab_0, slab_1, slab_2, slab_3)):
@@ -138,7 +137,12 @@
         both = k + pltpu.roll(f, HALO, 1)
         sent = sent + pltpu.roll(both, 2 * HALO * ((q - far) & 3), 1)
     out_ref[0:64] = sent
-    out_ref[64:72] = jnp.where(q == 3, profile_ref[3], profile_ref[0])
+    sent = jnp.zeros((64, 128), F32)
+    for j in range(8):
+        x = tile[1, pl.ds(j, 64, stride=8), :]
+        x = jnp.where(n < HALO, jnp.where(q == 3, pltpu.roll(x, HALO, 1), x), 0.0)
+        sent = sent + (pltpu.roll(x, 16 * j, 1) if j else x)
+    out_ref[64:128] = sent
 
 
 def halo_from(near, g, first):
@@ -163,16 +167,19 @@
         self.count, self.forward = count, forward
         self.order = range(count) if forward else range(count - 1, -1, -1)
 
-    def prepare(self, parts):
-        one = 1 if self.forward else -1
-        self.steps = []
+    def multiply(self, parts):
         for p in range(parts):
             running = None
             for t in self.order:
                 g = self.gains[p, t]
                 running = g if running is None else running * g
                 self.prefix[p, t] = running
-            a = shifted(running, one)
+
+    def prepare(self, parts):
+        one = 1 if self.forward else -1
+        self.steps = []
+        for p in range(parts):
+            a = shifted(self.prefix[p, self.order[-1]], one)
             steps = []
             for d in (1, 2, 4):
                 steps.append(a)
@@ -219,26 +226,13 @@
     return beside(ref, t, TC, forward, 0) + pltpu.roll(own, 1, 1) + pltpu.roll(own, 127, 1)
 
 
-SOLVE_SCRATCH = [
-    pltpu.VMEM((2, T, 8, 128), F32),
-    pltpu.VMEM((2, T, 8, 128), F32),
-    pltpu.VMEM((2, T, 8, 128), F32),
-    pltpu.VMEM((2, T, 8, 128), F32),
-    pltpu.VMEM((2, T, 8, 128), F32),
-    pltpu.VMEM((2, T, 8, 128), F32),
-    pltpu.VMEM((1, TC, 8, 128), F32),
-    pltpu.VMEM((1, TC, 8, 128), F32),
-    pltpu.VMEM((1, TC, 8, 128), F32),
-    pltpu.VMEM((1, TC, 8, 128), F32),
-    pltpu.VMEM((1, TC, 8, 128), F32),
-    pltpu.VMEM((1, TC, 8, 128), F32),
-    pltpu.VMEM((1, TC, 8, 128), F32),
-]
-
-
-def solve_on_slab(kf, source, scratch, forward, finish):
-    (gains, prefix, partial, scale, field, kept, cgains, cprefix, cpartial, cscale, ck, cfield,
-     csource) = scratch
+STENCIL_SHAPES = [(2, T, 8, 128)] * 3 + [(1, TC, 8, 128)] * 4
+WORK_SHAPES = [(2, T, 8, 128)] * 3 + [(1, TC, 8, 128)] * 3
+SOLVE_SCRATCH = [pltpu.VMEM(dims, F32) for dims in STENCIL_SHAPES + WORK_SHAPES]
+
+
+def build_stencils(kf, stencils, sums, forward):
+    gains, prefix, scale, cgains, cprefix, cscale, ck = stencils
     for c in range(TC):
         ksum = fsum = None
         for t in (2 * c, 2 * c + 1):
@@ -261,14 +255,21 @@
         fc = 0.5 * fsum
         inverse = 1.0 / (4.0 * kc + fc + 4.0 * SIGMA)
         ck[0, c] = kc
-        cfield[0, c] = kc + fc
+        sums[0, c] = kc + fc
         cscale[0, c] = inverse
     for c in range(TC):
         if forward:
-            cgains[0, c] = cfield[0, c] * cscale[0, c]
+            cgains[0, c] = sums[0, c] * cscale[0, c]
         else:
-            up = cfield[0, c + 1] if c + 1 < TC else shifted(cfield[0, 0], -1)
+            up = sums[0, c + 1] if c + 1 < TC else shifted(sums[0, 0], -1)
             cgains[0, c] = up * cscale[0, c]
+    Level(gains, prefix, None, T, forward).multiply(2)
+    Level(cgains, cprefix, None, TC, forward).multiply(1)
+
+
+def solve_on_slab(kf, source, stencils, work, forward, finish):
+    gains, prefix, scale, cgains, cprefix, cscale, ck = stencils
+    partial, field, kept, cpartial, cfield, csource = work
     fine = Level(gains, prefix, partial, T, forward)
     fine.prepare(2)
     coarse = Level(cgains, cprefix, cpartial, TC, forward)
@@ -345,8 +346,13 @@
 
 
 def forward_kernel(
-    place_ref, slab_0, slab_1, slab_2, slab_3, own_ref, near_ref, out_ref, kf_ref, natural, *scratch
+    place_ref, slab_0, slab_1, slab_2, slab_3, near_ref, heard_ref, tile,
+    out_ref, kf_ref, slot_ref, natural, *scratch,
 ):
+    heard = heard_ref[...]
+    for side, other in enumerate((place_ref[1] - 1, place_ref[1] + 1)):
+        told = jnp.sum(jnp.where(sub((64, 128)) == other, heard, 0.0), axis=0, keepdims=True)
+        slot_ref[side : side + 1] = pltpu.roll(told, 64, 1).astype(jnp.int32)
     q = place_ref[0]
     outer = near_ref[0:64]
     chosen = [to_pairs_matrix(2 * HALO * field) for field in range(2)]
@@ -363,24 +369,43 @@
         for p in range(2):
             for t in range(T):
                 kf_ref[2 * field + p, t] = natural[2 * field + p, pl.ds(t, 8, stride=T), :]
-    low = jnp.where(q == 0, near_ref[64:72], own_ref[jnp.maximum(q - 1, 0)])
-    high = jnp.where(q == 3, near_ref[64:72], own_ref[jnp.minimum(q + 1, 3)])
-    parts = edge_tile(low, high, HALO)
-    profile = select_dot(
-        jnp.concatenate([own_ref[q], parts[0] + parts[1]], axis=1), to_pairs_matrix(0)
-    )
+    steps = [jnp.broadcast_to(heard[:, j : j + 1], (64, 128)) for j in range(8)]
+    n = lane((64, 128))
+    pattern = jnp.zeros((64, 128), F32)
+    for j in range(8):
+        pattern = jnp.where((n >> 4) == j, steps[j], pattern)
+    folded = jnp.sum(near_ref[64:128] * pattern, axis=0, keepdims=True)
+    folded = jnp.broadcast_to(folded, (8, 128))
+    outside = folded
+    for j in range(1, 8):
+        outside = outside + pltpu.roll(folded, 128 - 16 * j, 1)
+    inside = []
+    for i in range(3):
+        total = jnp.zeros((64, 128), F32)
+        for j in range(8):
+            total = total + steps[j] * tile[i, pl.ds(j, 64, stride=8), :]
+        inside.append(jnp.broadcast_to(jnp.sum(total, axis=0, keepdims=True), (8, 128)))
+    n = lane((8, 128))
+    low = jnp.where(q == 0, outside, pltpu.roll(inside[0], HALO, 1))
+    high = pltpu.roll(jnp.where(q == 3, outside, inside[2]), HALO, 1)
+    ends = jnp.where(n < HALO, low, jnp.where(n < 2 * HALO, high, 0.0))
+    profile = select_dot(jnp.concatenate([inside[1], ends], axis=1), chosen[0])
     profile = jnp.where(sub((8, 256)) == 0, profile, 0.0)
     begin = []
     for p in range(2):
         k, f = kf_ref[p, 0], kf_ref[2 + p, 0]
         begin.append((k + f) * profile[:, 128 * p : 128 * p + 128] / (4.0 * k + f + SIGMA))
-    result = scratch[2]
+    stencils, work = scratch[:7], scratch[7:]
+    build_stencils(kf_ref, stencils, work[4], True)
+    result = work[2]
 
     def finish(t, values):
         for p in range(2):
             result[p, t] = values[p]
 
-    solve_on_slab(kf_ref, lambda t: tuple(begin) if t == 0 else None, scratch, True, finish)
+    solve_on_slab(
+        kf_ref, lambda t: tuple(begin) if t == 0 else None, stencils, work, True, finish
+    )
     chosen = from_pairs_matrix()
     both = jnp.concatenate(
         [result[0].reshape(256, 128), result[1].reshape(256, 128)], axis=1
@@ -444,11 +469,12 @@
             out_ref[width * (u - 1) + SLOTS + 1] = jnp.sum(first, axis=0, keepdims=True)
 
 
-def driving_kernel(slot_ref, near_ref, in_ref, out_ref, ends):
+def driving_kernel(place_ref, slot_ref, near_ref, in_ref, *rest):
+    outs, (blocks, ends) = rest[:4], rest[4:]
     for i in range(256):
         r, q = divmod(i, 4)
         at = slot_ref[i]
-        out_ref[q, 0, r : r + 1] = in_ref[at + 2 * (at >> 3)]
+        blocks[q, r : r + 1] = in_ref[at + 2 * (at >> 3)]
     for side in range(2):
         for r in range(64):
             at = near_ref[side, r]
@@ -456,26 +482,35 @@
             turn = (128 - 16 * (at & 7) + HALO * side) & 127
             ends[side, r : r + 1] = pltpu.roll(row, turn, 1)
     n = lane((64, 128))
-    for q in range(4):
-        low, high = edge_tile(out_ref[max(q - 1, 0), 0], out_ref[min(q + 1, 3), 0], HALO)
-        if q == 0:
-            low = jnp.where(n < HALO, ends[0], 0.0)
-        if q == 3:
-            high = jnp.where((n >= HALO) & (n < 2 * HALO), ends[1], 0.0)
-        out_ref[q, 1] = low + high
-
-
-def adjoint_kernel(place_ref, in_ref, kf_ref, modes_ref, out_ref, tile, natural, begin, *scratch):
+    for far in range(4):
+        q = (place_ref[0] + far) & 3
+        low, high = edge_tile(
+            blocks[jnp.maximum(q - 1, 0)], blocks[jnp.minimum(q + 1, 3)], HALO
+        )
+        low = jnp.where(q == 0, jnp.where(n < HALO, ends[0], 0.0), low)
+        high = jnp.where(
+            q == 3, jnp.where((n >= HALO) & (n < 2 * HALO), ends[1], 0.0), high
+        )
+        outs[far][0] = blocks[q]
+        outs[far][1] = low + high
+
+
+def stencil_kernel(kf_ref, after_ref, *rest):
+    build_stencils(kf_ref, rest[:7], rest[7], False)
+
+
+def adjoint_kernel(place_ref, tile, kf_ref, *rest):
+    slabs, stencils, rest = rest[:4], rest[4:11], rest[11:]
+    out_ref, natural, begin, *work = rest
     chosen = to_pairs_matrix(0)
-    for g in range(4):
-        x = jnp.concatenate([in_ref[g, 0], in_ref[g, 1]], axis=1)
-        got = select_dot(x, chosen)
-        natural[0, 64 * g : 64 * g + 64] = got[:, :128]
-        natural[1, 64 * g : 64 * g + 64] = got[:, 128:]
+    for far, slab in enumerate(slabs):
+        got = select_dot(jnp.concatenate([slab[0], slab[1]], axis=1), chosen)
+        rows = pl.ds(pl.multiple_of(64 * ((place_ref[0] - far) & 3), 64), 64)
+        natural[0, rows, :] = got[:, :128]
+        natural[1, rows, :] = got[:, 128:]
     for p in range(2):
         for t in range(T):
-            k, f = kf_ref[p, t], kf_ref[2 + p, t]
-            begin[p, t] = natural[p, pl.ds(t, 8, stride=T), :] / (4.0 * k + f + SIGMA)
+            begin[p, t] = natural[p, pl.ds(t, 8, stride=T), :] * stencils[2][p, t]
     flux = []
 
     def finish(t, values):
@@ -483,14 +518,14 @@
             for p in range(2):
                 flux.append((kf_ref[p, 0] + kf_ref[2 + p, 0]) * values[p])
 
-    solve_on_slab(kf_ref, lambda t: (begin[0, t], begin[1, t]), scratch, False, finish)
+    solve_on_slab(
+        kf_ref, lambda t: (begin[0, t], begin[1, t]), stencils, work, False, finish
+    )
     natural_flux = select_dot(jnp.concatenate(flux, axis=1), from_pairs_matrix())
     row = natural_flux[0:1]
     out = jnp.zeros((256, 128), F32)
-    column = pl.multiple_of(place_ref[0] * 128, 128)
-    tile[...] = modes_ref[:, pl.ds(column, 128)]
     for j in range(2):
-        modes = tile[pl.ds(j, 256, stride=2), :]
+        modes = tile[1, pl.ds(j, 256, stride=2), :]
         part = jnp.sum(modes * row, axis=1, keepdims=True)
         out = jnp.where(lane((256, 128)) == j, part, out)
     out_ref[...] = out
@@ -498,26 +533,26 @@
 
 VM = pl.BlockSpec(memory_space=pltpu.VMEM)
 SM = pl.BlockSpec(memory_space=pltpu.SMEM)
+FAR = pl.BlockSpec(memory_space=pltpu.HBM)
 PARAMS = pltpu.CompilerParams(vmem_limit_bytes=16 << 20)
-
-
-def near(array):
-    return pltpu.with_memory_space_constraint(array, pltpu.VMEM)
 
 
 def held(*dims, dtype=F32):
     return pltpu.VMEM(dims, dtype)
 
 
-def run(kernel, name, ins, outs, scratch=(), pinned=True):
-    scalars = [array.dtype == jnp.int32 and name != "prepare" for array in ins]
-    scalars[0] = ins[0].dtype == jnp.int32
-    specs = [SM if scalar else VM if pinned else pl.BlockSpec() for scalar in scalars]
-    if pinned:
-        ins = [array if scalar else near(array) for array, scalar in zip(ins, scalars)]
-    else:
-        ins = [array if scalar else pltpu.with_memory_space_constraint(array, pltpu.HBM)
-               for array, scalar in zip(ins, scalars)]
+def run(kernel, name, ins, outs, scratch=(), far=()):
+    specs, placed = [], []
+    for i, array in enumerate(ins):
+        if array.dtype == jnp.int32 and i not in far:
+            specs.append(SM)
+        elif i in far:
+            specs.append(pl.BlockSpec() if i < 6 else FAR)
+            array = pltpu.with_memory_space_constraint(array, pltpu.HBM)
+        else:
+            specs.append(VM)
+            array = pltpu.with_memory_space_constraint(array, pltpu.VMEM)
+        placed.append(array)
     return pl.pallas_call(
         kernel,
         in_specs=specs,
@@ -526,7 +561,7 @@
         scratch_shapes=list(scratch),
         compiler_params=PARAMS,
         name=name,
-    )(*ins)
+    )(*placed)
 
 
 def exchange(array, axis):
@@ -546,7 +581,7 @@
     count = lax.axis_size("sub")
     place = jnp.stack([lax.axis_index("seg"), lax.axis_index("sub")]).astype(jnp.int32)
 
-    *slab, message, slots = run(
+    *slab, message, slots, tile = run(
         prepare_kernel,
         "prepare",
         (
@@ -556,32 +591,36 @@
             brick_owner.reshape(1, 256),
             voxel_row.reshape(1, 256),
             profile_step.reshape(1, 8),
+            inlet_modes,
         ),
-        (held(3, 64, 128),) * 4 + (held(64, 128), held(1, 256, dtype=jnp.int32)),
-        pinned=False,
+        (held(3, 64, 128),) * 4
+        + (held(64, 128), held(1, 256, dtype=jnp.int32), held(3, 512, 128)),
+        [pltpu.SemaphoreType.DMA((3,))],
+        far=(1, 2, 3, 4, 5, 6),
     )
     slots = slots.reshape(256)
     for far in (2, 1, 3):
         slab[far] = lax.ppermute(slab[far], "seg", [(i, (i + far) % 4) for i in range(4)])
-    heard = exchange(message.reshape(count, 1, 128), "sub").reshape(count, 128)
-
-    own_profile, near_slots, to_near = run(
+    to_near, message = run(
         border_kernel,
         "border",
-        (place, heard, inlet_modes, *slab),
-        (held(4, 8, 128), held(2, 128, dtype=jnp.int32), held(72, 128)),
-        [pltpu.VMEM((4, 512, 128), F32)],
+        (place, tile, message, *slab),
+        (held(128, 128), held(64, 128)),
     )
     outward = [(3 * count + i, i + 1) for i in range(count - 1)]
     outward += [(i + 1, 3 * count + i) for i in range(count - 1)]
     from_near = lax.ppermute(to_near, ALL, outward)
-
-    field, kf = run(
+    heard = exchange(message.reshape(count, 1, 128), "sub").reshape(count, 128)
+
+    field, kf, near_slots = run(
         forward_kernel,
         "forward",
-        (place, *slab, own_profile, from_near),
-        (held(256, 128), held(4, T, 8, 128)),
-        [pltpu.VMEM((4, 256, 128), F32)] + SOLVE_SCRATCH,
+        (place, *slab, from_near, heard, tile),
+        (held(256, 128), held(4, T, 8, 128), held(2, 128, dtype=jnp.int32)),
+        [
+            pltpu.VMEM((4, 256, 128), F32),
+        ]
+        + SOLVE_SCRATCH,
     )
     back = exchange(field.reshape(4, 64, 128), "seg")
 
@@ -598,26 +637,36 @@
     )
     answered = exchange(answer, "sub")
 
-    (spread,) = run(
+    slab = run(
         driving_kernel,
         "driving",
-        (slots, near_slots, answered),
-        (held(4, 2, 64, 128),),
-        [pltpu.VMEM((2, 64, 128), F32)],
-    )
-    slab = exchange(spread, "seg")
+        (place, slots, near_slots, answered),
+        (held(2, 64, 128),) * 4,
+        [pltpu.VMEM((4, 64, 128), F32), pltpu.VMEM((2, 64, 128), F32)],
+    )
+    sent = slab[0]
+    slab = [sent] + [
+        lax.ppermute(slab[far], "seg", [(i, (i + far) % 4) for i in range(4)])
+        for far in (1, 2, 3)
+    ]
+    stencils = run(
+        stencil_kernel,
+        "stencils",
+        (kf, sent),
+        tuple(held(*dims) for dims in STENCIL_SHAPES),
+        [pltpu.VMEM((1, TC, 8, 128), F32)],
+    )
 
     (partial,) = run(
         adjoint_kernel,
         "adjoint",
-        (place, slab, kf, inlet_modes),
+        (place, tile, kf, *slab, *stencils),
         (held(256, 128),),
         [
-            pltpu.VMEM((512, 128), F32),
             pltpu.VMEM((2, 256, 128), F32),
             pltpu.VMEM((2, T, 8, 128), F32),
         ]
-        + SOLVE_SCRATCH,
+        + [pltpu.VMEM(dims, F32) for dims in WORK_SHAPES],
     )
     gathered = exchange(partial.reshape(256, 1, 128), ALL)
     product = jnp.sum(gathered, axis=(0, 1))[:2]

time: 126 us -> 123 us (0.976)
  blocking collectives: 78.7 us -> 64.7 us
  starting transfers between devices: 14.4 us -> 22.9 us
  waiting for transfers between devices: 15.9 us -> 18 us
  Pallas kernels: 12.3 us -> 13.8 us
    all_to_all x5 -> x4, blocking collectives: 78.7 us -> 64.7 us  [exchange(): return lax.all_to_all(array, axis, split_axis=0, concat_axis=0, tiled=True)]
    ppermute x3 -> x6, waiting for transfers between devices: 0.01 us -> 6.5 us  [on_device(): lax.ppermute(slab[far], 'seg', [(i, (i + far) % 4) for i in range(4)])]
    ppermute x1, waiting for transfers between devices: 4.28 us -> 0.01 us  [on_device(): from_near = lax.ppermute(to_near, ALL, outward)]
    ppermute x1, starting transfers between devices: 2.19 us -> 6.42 us  [on_device(): from_near = lax.ppermute(to_near, ALL, outward)]
    ppermute x3 -> x6, starting transfers between devices: 5.88 us -> 8.74 us  [on_device(): lax.ppermute(slab[far], 'seg', [(i, (i + far) % 4) for i in range(4)])]
    pallas_call x7 -> x8, Pallas kernels: 12.3 us -> 13.8 us  [run(): pl.pallas_call(kernel, in_specs=specs, out_specs=[VM] * len(outs), out_sh...]
    all_to_all x1, starting transfers between devices: 6.28 us -> 7.72 us  [exchange(): return lax.all_to_all(array, axis, split_axis=0, concat_axis=0, tiled=True)]
  transfers between devices with their start and end apart: 5 -> 8, of which waited for: 2 -> 5; matrix products, arithmetic and copies ran while one was open for 1% -> 1% of each run, Pallas kernels for 0% -> 0%
where the time goes in v2:
time: 123 us; the launch traced here: 122 us
  blocking collectives  64.7 us (53%)
  starting transfers between devices  22.9 us (19%)
  waiting for transfers between devices  18 us (15%)
  Pallas kernels  13.8 us (11%)
  local copies, waits for them, and re-layouts  1.27 us (1%)
    all_to_all x4, blocking collectives, exchange(): return lax.all_to_all(array, axis, split_axis=0, concat_axis=0, tiled=True)  64.7 us
    pallas_call x8, Pallas kernels, run(): pl.pallas_call(kernel, in_specs=specs, out_specs=[VM] * len(outs), out_sh...  13.8 us
    all_to_all x1, waiting for transfers between devices, exchange(): return lax.all_to_all(array, axis, split_axis=0, concat_axis=0, tiled=True)  11.5 us
    ppermute x6, starting transfers between devices, on_device(): lax.ppermute(slab[far], 'seg', [(i, (i + far) % 4) for i in range(4)])  8.74 us
    all_to_all x1, starting transfers between devices, exchange(): return lax.all_to_all(array, axis, split_axis=0, concat_axis=0, tiled=True)  7.72 us
    ppermute x6, waiting for transfers between devices, on_device(): lax.ppermute(slab[far], 'seg', [(i, (i + far) % 4) for i in range(4)])  6.5 us
    ppermute x1, starting transfers between devices, on_device(): from_near = lax.ppermute(to_near, ALL, outward)  6.42 us
  transfers between devices with their start and end apart: 8, of which 5 were waited for; matrix products, arithmetic and copies ran while one was open for 1% of the time, Pallas kernels for 0%

profile of v2, /device:TPU:1, one launch (start us, length us, event | category | flops | bytes accessed | tf_op | source)
XLA Modules:
  0.0 122.2 jit_solution(13147223830785538140)
XLA Ops:
  0.6 0.1 pad_add_fusion.place_ref
  0.7 2.5 %prepare.1 = (f32[3,64,128]{2,1,0:T(8,128)S(1)}, f32[3,64,128]{2,1,0:T(8,128)S(1)}, f32[3,64,128]{2,1,0:T(8,128)S(1)}, f32[3,64,128]{2,1,0:T(8,128)S(1)}, f32[64...) custom-call(s32[2]{0:T(128)S(1)} %pad_add_fusion.place_ref, f32[64,512]{1,0:T(8,128)} %k_ref.1, ...), custom_call_target="tpu_custom_call" | custom-call | tf_op jit(solution)/shard_map/prepare/pallas_call | solution.py:556
  3.3 2.2 %collective-permute-start = (f32[3,64,128]{2,1,0:T(8,128)S(1)}, f32[3,64,128]{2,1,0:T(8,128)S(1)}, u32[]{:S(2)}, u32[]{:S(2)}) collective-permute-start(f32[3,64,128]{2,1,0:T(8,128)S(1)} %get-tuple-element.32), channel_id=1, source_target_pairs={{0,64},{64,128},{128,192},{192,0},{1,65},{65,129},{129,193},{193,1... | collective-permute-start | bytes 294920 | tf_op jit(solution)/shard_map/ppermute | solution.py:603
  5.5 2.6 %collective-permute-start.1 = (f32[3,64,128]{2,1,0:T(8,128)S(1)}, f32[3,64,128]{2,1,0:T(8,128)S(1)}, u32[]{:S(2)}, u32[]{:S(2)}) collective-permute-start(f32[3,64,128]{2,1,0:T(8,128)S(1)} %get-tuple-element.33), channel_id=1, source_target_pairs={{0,128},{64,192},{128,0},{192,64},{1,129},{65,193},{129,1},{193,65... | collective-permute-start | bytes 294920 | tf_op jit(solution)/shard_map/ppermute | solution.py:603
  8.1 1.0 collective-permute-start.2
  9.1 0.0 collective-permute-done.slab_1
  9.1 3.0 %collective-permute-done.1.slab_2 = f32[3,64,128]{2,1,0:T(8,128)S(1)} collective-permute-done((f32[3,64,128]{2,1,0:T(8,128)S(1)}, f32[3,64,128]{2,1,0:T(8,128)S(1)}, u32[]{:S(2)}, u32[]{:S(2)}) %collective-permute-start.1) | collective-permute-done | bytes 98336 | tf_op jit(solution)/shard_map/ppermute | solution.py:603
  12.1 0.0 collective-permute-done.2.slab_3
  12.1 1.2 border.1
  13.3 6.4 %collective-permute-start.3 = (f32[128,128]{1,0:T(8,128)S(1)}, f32[128,128]{1,0:T(8,128)S(1)}, u32[]{:S(2)}, u32[]{:S(2)}) collective-permute-start(f32[128,128]{1,0:T(8,128)S(1)} %get-tuple-element.37), channel_id=1, source_target_pairs={{192,1},{193,2},{194,3},{195,4},{196,5},{197,6},{198,7},{199,8},{2... | collective-permute-start | bytes 196616 | tf_op jit(solution)/shard_map/ppermute | solution.py:612
  19.8 20.3 %all_to_all.25 = f32[64,1,128]{2,1,0:T(1,128)S(1)} all-to-all(f32[64,1,128]{2,1,0:T(1,128)S(1)} %bitcast.22), channel_id=1, replica_groups=mesh['seg'=4,'sub'=64] {'sub'}, dimensions={0} | all-to-all | bytes 65536 | tf_op jit(solution)/shard_map/all_to_all | solution.py:568
  40.0 0.0 collective-permute-done.3.near_ref
  40.0 3.4 %forward.1 = (f32[256,128]{1,0:T(8,128)S(1)}, f32[4,32,8,128]{3,2,1,0:T(8,128)S(1)}, s32[2,128]{1,0:T(2,128)S(1)}) custom-call(s32[2]{0:T(128)S(1)} %pad_add_fusion.place_ref, f32[3,64,128]{2,1,0:T(8,128)S(1)} %get-tuple-element.31.slab_0, f32[3,64,128]{2,1,0:T(8,128)S(1)} %collective-permute-done.slab_1, f32[3,64,128]{2,1,0:T(8,128)S(1)} %collective-permute-done.1.slab_2, ...), custom_call_target="tpu_custom_call" | custom-call | tf_op jit(solution)/shard_map/forward/pallas_call | solution.py:556
  43.4 7.2 %all_to_all.26.in_ref = f32[4,64,128]{2,1,0:T(8,128)S(1)} all-to-all(f32[4,64,128]{2,1,0:T(8,128)S(1)} %bitcast.21), channel_id=1, replica_groups=mesh['seg'=4,'sub'=64] {'seg'}, dimensions={0} | all-to-all | bytes 262144 | tf_op jit(solution)/shard_map/all_to_all | solution.py:568
  50.6 0.7 pack.1
  51.3 0.0 copy-start
  51.3 0.0 copy-start.1
  51.3 18.4 %all_to_all.27 = f32[64,8,128]{2,1,0:T(8,128)S(1)} all-to-all(f32[64,8,128]{2,1,0:T(8,128)S(1)} %bitcast.20), channel_id=1, replica_groups=mesh['seg'=4,'sub'=64] {'sub'}, dimensions={0} | all-to-all | bytes 524288 | tf_op jit(solution)/shard_map/all_to_all | solution.py:568
  69.7 0.0 copy-done
  69.7 0.0 copy-done.1
  69.7 1.3 %voxels.1 = (f32[16,128]{1,0:T(8,128)S(1)}, f32[640,1,128]{2,1,0:T(1,128)S(1)}) custom-call(f32[512,128]{1,0:T(8,128)S(1)} %bitcast.17, f32[64,128]{1,0:T(8,128)S(1)} %bitcast.19, f32[16,128]{1,0:T(8,128)S(1)} %copy-done.1, f32[128,128]{1,0:T(8,128)S(1)} %copy-done), custom_call_target="tpu_custom_call" | custom-call | tf_op jit(solution)/shard_map/voxels/pallas_call | solution.py:556
  71.0 18.8 %all_to_all.28.in_ref = f32[640,1,128]{2,1,0:T(1,128)S(1)} all-to-all(f32[640,1,128]{2,1,0:T(1,128)S(1)} %get-tuple-element.45), channel_id=1, replica_groups=mesh['seg'=4,'sub'=64] {'sub'}, dimensions={0} | all-to-all | bytes 655360 | tf_op jit(solution)/shard_map/all_to_all | solution.py:568
  89.9 1.3 %driving.1 = (f32[2,64,128]{2,1,0:T(8,128)S(1)}, f32[2,64,128]{2,1,0:T(8,128)S(1)}, f32[2,64,128]{2,1,0:T(8,128)S(1)}, f32[2,64,128]{2,1,0:T(8,128)S(1)}) custom-call(s32[2]{0:T(128)S(1)} %pad_add_fusion.place_ref, s32[256]{0:T(256)S(1)} %bitcast.24, s32[2,128]{1,0:T(2,128)S(1)} %get-tuple-element.44.near_ref, f32[640,1,128]{2,1,0:T(1,128)S(1)} %all_to_all.28.in_ref), custom_call_target="tpu_custom_call" | custom-call | tf_op jit(solution)/shard_map/driving/pallas_call | solution.py:556
  91.2 0.4 collective-permute-start.4
  91.6 1.8 %collective-permute-start.5 = (f32[2,64,128]{2,1,0:T(8,128)S(1)}, f32[2,64,128]{2,1,0:T(8,128)S(1)}, u32[]{:S(2)}, u32[]{:S(2)}) collective-permute-start(f32[2,64,128]{2,1,0:T(8,128)S(1)} %get-tuple-element.48), channel_id=1, source_target_pairs={{0,128},{64,192},{128,0},{192,64},{1,129},{65,193},{129,1},{193,65... | collective-permute-start | bytes 196616 | tf_op jit(solution)/shard_map/ppermute | solution.py:649
  93.3 0.7 collective-permute-start.6
  94.0 0.1 stencils.1
  94.2 2.0 %collective-permute-done.4.rest_1_ = f32[2,64,128]{2,1,0:T(8,128)S(1)} collective-permute-done((f32[2,64,128]{2,1,0:T(8,128)S(1)}, f32[2,64,128]{2,1,0:T(8,128)S(1)}, u32[]{:S(2)}, u32[]{:S(2)}) %collective-permute-start.4) | collective-permute-done | bytes 65568 | tf_op jit(solution)/shard_map/ppermute | solution.py:649
  96.2 0.5 collective-permute-done.5.rest_2_
  96.7 1.0 collective-permute-done.6.rest_3_
  97.7 3.2 %adjoint.1 = f32[256,128]{1,0:T(8,128)} custom-call(s32[2]{0:T(128)S(1)} %pad_add_fusion.place_ref, f32[3,512,128]{2,1,0:T(8,128)S(1)} %get-tuple-element.35.tile, f32[4,32,8,128]{3,2,1,0:T(8,128)S(1)} %get-tuple-element.43.kf_ref, f32[2,64,128]{2,1,0:T(8,128)S(1)} %get-tuple-element.46.after_ref.rest_0_, f32[2,64,128]{2,1,0:T(8,128)S(1)} %collective-permute-done.4.rest_1_, ...), custom_call_target="tpu_custom_call" | custom-call | tf_op jit(solution)/shard_map/adjoint/pallas_call | solution.py:556
  100.9 7.7 %all-to-all-start.4 = ((f32[256,1,128]{2,1,0:T(1,128)}), f32[256,1,128]{2,1,0:T(1,128)S(1)}, u32[]{:S(2)}, u32[]{:S(2)}) async-start(f32[256,1,128]{2,1,0:T(1,128)} %bitcast.13), calls=%async_computation.4 | async-start | bytes 262144 | tf_op jit(solution)/shard_map/all_to_all | solution.py:568
  108.6 0.7 copy.13
  109.3 0.6 copy.14
  109.9 11.5 %all-to-all-done.4 = f32[256,1,128]{2,1,0:T(1,128)S(1)} async-done(((f32[256,1,128]{2,1,0:T(1,128)}), f32[256,1,128]{2,1,0:T(1,128)S(1)}, u32[]{:S(2)}, u32[]{:S(2)}) %all-to-all-start.4) | async-done | bytes 131104 | tf_op jit(solution)/shard_map/all_to_all | solution.py:568
  121.4 0.8 reduce_sum.9
Async XLA Ops:
  3.3 5.9 %collective-permute-start = (f32[3,64,128]{2,1,0:T(8,128)S(1)}, f32[3,64,128]{2,1,0:T(8,128)S(1)}, u32[]{:S(2)}, u32[]{:S(2)}) collective-permute-start(f32[3,64,128]{2,1,0:T(8,128)S(1)} %get-tuple-element.32), channel_id=1, source_target_pairs={{0,64},{64,128},{128,192},{192,0},{1,65},{65,129},{129,193},{193,1... | collective-permute-start | bytes 294920 | tf_op jit(solution)/shard_map/ppermute | solution.py:603
  5.5 6.7 %collective-permute-start.1 = (f32[3,64,128]{2,1,0:T(8,128)S(1)}, f32[3,64,128]{2,1,0:T(8,128)S(1)}, u32[]{:S(2)}, u32[]{:S(2)}) collective-permute-start(f32[3,64,128]{2,1,0:T(8,128)S(1)} %get-tuple-element.33), channel_id=1, source_target_pairs={{0,128},{64,192},{128,0},{192,64},{1,129},{65,193},{129,1},{193,65... | collective-permute-start | bytes 294920 | tf_op jit(solution)/shard_map/ppermute | solution.py:603
  8.1 4.0 %collective-permute-start.2 = (f32[3,64,128]{2,1,0:T(8,128)S(1)}, f32[3,64,128]{2,1,0:T(8,128)S(1)}, u32[]{:S(2)}, u32[]{:S(2)}) collective-permute-start(f32[3,64,128]{2,1,0:T(8,128)S(1)} %get-tuple-element.34), channel_id=1, source_target_pairs={{0,192},{64,0},{128,64},{192,128},{1,193},{65,1},{129,65},{193,129... | collective-permute-start | bytes 294920 | tf_op jit(solution)/shard_map/ppermute | solution.py:603
  13.3 26.7 %collective-permute-start.3 = (f32[128,128]{1,0:T(8,128)S(1)}, f32[128,128]{1,0:T(8,128)S(1)}, u32[]{:S(2)}, u32[]{:S(2)}) collective-permute-start(f32[128,128]{1,0:T(8,128)S(1)} %get-tuple-element.37), channel_id=1, source_target_pairs={{192,1},{193,2},{194,3},{195,4},{196,5},{197,6},{198,7},{199,8},{2... | collective-permute-start | bytes 196616 | tf_op jit(solution)/shard_map/ppermute | solution.py:612
  51.3 18.4 %copy-start = (f32[128,128]{1,0:T(8,128)S(1)}, f32[128,128]{1,0:T(8,128)}, u32[]{:S(2)}) copy-start(f32[128,128]{1,0:T(8,128)} %spread_ref.1) | copy-start | bytes 196612
  51.3 18.4 %copy-start.1 = (f32[16,128]{1,0:T(8,128)S(1)}, f32[16,128]{1,0:T(8,128)}, u32[]{:S(2)}) copy-start(f32[16,128]{1,0:T(8,128)} %weight_ref.1) | copy-start | bytes 24580
  91.2 5.0 %collective-permute-start.4 = (f32[2,64,128]{2,1,0:T(8,128)S(1)}, f32[2,64,128]{2,1,0:T(8,128)S(1)}, u32[]{:S(2)}, u32[]{:S(2)}) collective-permute-start(f32[2,64,128]{2,1,0:T(8,128)S(1)} %get-tuple-element.47), channel_id=1, source_target_pairs={{0,64},{64,128},{128,192},{192,0},{1,65},{65,129},{129,193},{193,1... | collective-permute-start | bytes 196616 | tf_op jit(solution)/shard_map/ppermute | solution.py:649
  91.6 5.2 %collective-permute-start.5 = (f32[2,64,128]{2,1,0:T(8,128)S(1)}, f32[2,64,128]{2,1,0:T(8,128)S(1)}, u32[]{:S(2)}, u32[]{:S(2)}) collective-permute-start(f32[2,64,128]{2,1,0:T(8,128)S(1)} %get-tuple-element.48), channel_id=1, source_target_pairs={{0,128},{64,192},{128,0},{192,64},{1,129},{65,193},{129,1},{193,65... | collective-permute-start | bytes 196616 | tf_op jit(solution)/shard_map/ppermute | solution.py:649
  93.3 4.3 %collective-permute-start.6 = (f32[2,64,128]{2,1,0:T(8,128)S(1)}, f32[2,64,128]{2,1,0:T(8,128)S(1)}, u32[]{:S(2)}, u32[]{:S(2)}) collective-permute-start(f32[2,64,128]{2,1,0:T(8,128)S(1)} %get-tuple-element.49), channel_id=1, source_target_pairs={{0,192},{64,0},{128,64},{192,128},{1,193},{65,1},{129,65},{193,129... | collective-permute-start | bytes 196616 | tf_op jit(solution)/shard_map/ppermute | solution.py:649
  100.9 20.5 %all-to-all-start.4 = ((f32[256,1,128]{2,1,0:T(1,128)}), f32[256,1,128]{2,1,0:T(1,128)S(1)}, u32[]{:S(2)}, u32[]{:S(2)}) async-start(f32[256,1,128]{2,1,0:T(1,128)} %bitcast.13), calls=%async_computation.4 | async-start | bytes 262144 | tf_op jit(solution)/shard_map/all_to_all | solution.py:568

commit v3 on v2

--- a/solution.py
+++ b/solution.py
@@ -72,18 +72,9 @@
 
 
 def prepare_kernel(
-    place_ref, k_ref, f_ref, owner_ref, row_ref, step_ref, modes_ref, *outs
+    place_ref, k_ref, f_ref, owner_ref, row_ref, step_ref, *outs
 ):
-    message_ref, slot_ref, tile, sems = outs[4:]
-    copies = []
-    for i in range(3):
-        start = 128 * jnp.clip(place_ref[0] + i - 1, 0, 3)
-        copies.append(
-            pltpu.make_async_copy(
-                modes_ref.at[:, pl.ds(pl.multiple_of(start, 128), 128)], tile.at[i], sems.at[i]
-            )
-        )
-        copies[-1].start()
+    message_ref, slot_ref = outs[4:]
     owner_row = owner_ref[...]
     owner = jnp.transpose(jnp.broadcast_to(owner_row.astype(F32), (8, 256)))[:, 0:1]
     row = jnp.transpose(jnp.broadcast_to(row_ref[...].astype(F32), (8, 256)))[:, 0:1]
@@ -112,13 +103,24 @@
         own = pl.ds(pl.multiple_of(128 * q, 128), 128)
         below = pl.ds(pl.multiple_of(128 * jnp.maximum(q - 1, 0), 128), 128)
         above = pl.ds(pl.multiple_of(128 * jnp.minimum(q + 1, 3), 128), 128)
-        outs[far][0] = k_ref[:, own]
-        outs[far][1] = f_ref[:, own]
+        outs[far][0:64] = k_ref[:, own]
+        outs[far][64:128] = f_ref[:, own]
         halo = jnp.zeros((64, 128), F32)
         for ref, shift in ((k_ref, HALO), (f_ref, 3 * HALO)):
             low, high = edge_tile(ref[:, below], ref[:, above], shift)
             halo = halo + jnp.where(q > 0, low, 0.0) + jnp.where(q < 3, high, 0.0)
-        outs[far][2] = halo
+        outs[far][128:160] = halo[0:32] + pltpu.roll(halo[32:64], 64, 1)
+
+def load_kernel(place_ref, modes_ref, after_ref, tile, sems):
+    copies = []
+    for i in range(3):
+        start = 128 * jnp.clip(place_ref[0] + i - 1, 0, 3)
+        copies.append(
+            pltpu.make_async_copy(
+                modes_ref.at[:, pl.ds(pl.multiple_of(start, 128), 128)], tile.at[i], sems.at[i]
+            )
+        )
+        copies[-1].start()
     for copy in copies:
         copy.wait()
 
@@ -131,7 +133,7 @@
     n = lane((64, 128))
     sent = jnp.zeros((64, 128), F32)
     for far, slab_ref in enumerate((slab_0, slab_1, slab_2, slab_3)):
-        k, f = slab_ref[0], slab_ref[1]
+        k, f = slab_ref[0:64], slab_ref[64:128]
         k = jnp.where(n < HALO, jnp.where(q == 3, pltpu.roll(k, HALO, 1), k), 0.0)
         f = jnp.where(n < HALO, jnp.where(q == 3, pltpu.roll(f, HALO, 1), f), 0.0)
         both = k + pltpu.roll(f, HALO, 1)
@@ -358,10 +360,12 @@
     chosen = [to_pairs_matrix(2 * HALO * field) for field in range(2)]
     for far, slab_ref in enumerate((slab_0, slab_1, slab_2, slab_3)):
         g = (q - far) & 3
-        halo = slab_ref[2] + halo_from(outer, g, q == 0)
+        halo = slab_ref[128:160]
+        halo = jnp.concatenate([halo, pltpu.roll(halo, 64, 1)], axis=0)
+        halo = jnp.where(lane((64, 128)) < 4 * HALO, halo, 0.0) + halo_from(outer, g, q == 0)
         rows = pl.ds(pl.multiple_of(64 * g, 64), 64)
         for field in range(2):
-            x = jnp.concatenate([slab_ref[field], halo], axis=1)
+            x = jnp.concatenate([slab_ref[64 * field : 64 * field + 64], halo], axis=1)
             got = select_dot(x, chosen[field])
             natural[2 * field, rows, :] = got[:, :128]
             natural[2 * field + 1, rows, :] = got[:, 128:]
@@ -491,8 +495,12 @@
         high = jnp.where(
             q == 3, jnp.where((n >= HALO) & (n < 2 * HALO), ends[1], 0.0), high
         )
-        outs[far][0] = blocks[q]
-        outs[far][1] = low + high
+        outs[far][0:64] = blocks[q]
+        halo = low + high
+        packed = halo[0:16]
+        for g in range(1, 4):
+            packed = packed + pltpu.roll(halo[16 * g : 16 * g + 16], 32 * g, 1)
+        outs[far][64:80] = packed
 
 
 def stencil_kernel(kf_ref, after_ref, *rest):
@@ -504,7 +512,10 @@
     out_ref, natural, begin, *work = rest
     chosen = to_pairs_matrix(0)
     for far, slab in enumerate(slabs):
-        got = select_dot(jnp.concatenate([slab[0], slab[1]], axis=1), chosen)
+        packed = slab[64:80]
+        halo = [packed] + [pltpu.roll(packed, 128 - 32 * g, 1) for g in range(1, 4)]
+        halo = jnp.concatenate(halo, axis=0)
+        got = select_dot(jnp.concatenate([slab[0:64], halo], axis=1), chosen)
         rows = pl.ds(pl.multiple_of(64 * ((place_ref[0] - far) & 3), 64), 64)
         natural[0, rows, :] = got[:, :128]
         natural[1, rows, :] = got[:, 128:]
@@ -531,6 +542,10 @@
     out_ref[...] = out
 
 
+def total_kernel(in_ref, out_ref):
+    out_ref[...] = jnp.sum(in_ref[...], axis=0, keepdims=True)[:, 0:2]
+
+
 VM = pl.BlockSpec(memory_space=pltpu.VMEM)
 SM = pl.BlockSpec(memory_space=pltpu.SMEM)
 FAR = pl.BlockSpec(memory_space=pltpu.HBM)
@@ -547,7 +562,7 @@
         if array.dtype == jnp.int32 and i not in far:
             specs.append(SM)
         elif i in far:
-            specs.append(pl.BlockSpec() if i < 6 else FAR)
+            specs.append(pl.BlockSpec() if name == "prepare" else FAR)
             array = pltpu.with_memory_space_constraint(array, pltpu.HBM)
         else:
             specs.append(VM)
@@ -556,7 +571,7 @@
     return pl.pallas_call(
         kernel,
         in_specs=specs,
-        out_specs=[VM] * len(outs),
+        out_specs=[pl.BlockSpec() if name == "total" else VM] * len(outs),
         out_shape=outs,
         scratch_shapes=list(scratch),
         compiler_params=PARAMS,
@@ -581,7 +596,7 @@
     count = lax.axis_size("sub")
     place = jnp.stack([lax.axis_index("seg"), lax.axis_index("sub")]).astype(jnp.int32)
 
-    *slab, message, slots, tile = run(
+    *slab, message, slots = run(
         prepare_kernel,
         "prepare",
         (
@@ -591,14 +606,19 @@
             brick_owner.reshape(1, 256),
             voxel_row.reshape(1, 256),
             profile_step.reshape(1, 8),
-            inlet_modes,
         ),
-        (held(3, 64, 128),) * 4
-        + (held(64, 128), held(1, 256, dtype=jnp.int32), held(3, 512, 128)),
+        (held(160, 128),) * 4 + (held(64, 128), held(1, 256, dtype=jnp.int32)),
+        far=(1, 2, 3, 4, 5),
+    )
+    slots = slots.reshape(256)
+    (tile,) = run(
+        load_kernel,
+        "load",
+        (place, inlet_modes, slab[0]),
+        (held(3, 512, 128),),
         [pltpu.SemaphoreType.DMA((3,))],
-        far=(1, 2, 3, 4, 5, 6),
-    )
-    slots = slots.reshape(256)
+        far=(1,),
+    )
     for far in (2, 1, 3):
         slab[far] = lax.ppermute(slab[far], "seg", [(i, (i + far) % 4) for i in range(4)])
     to_near, message = run(
@@ -641,7 +661,7 @@
         driving_kernel,
         "driving",
         (place, slots, near_slots, answered),
-        (held(2, 64, 128),) * 4,
+        (held(80, 128),) * 4,
         [pltpu.VMEM((4, 64, 128), F32), pltpu.VMEM((2, 64, 128), F32)],
     )
     sent = slab[0]
@@ -669,7 +689,10 @@
         + [pltpu.VMEM(dims, F32) for dims in WORK_SHAPES],
     )
     gathered = exchange(partial.reshape(256, 1, 128), ALL)
-    product = jnp.sum(gathered, axis=(0, 1))[:2]
+    (product,) = run(
+        total_kernel, "total", (gathered.reshape(256, 128),), (jax.ShapeDtypeStruct((1, 2), F32),)
+    )
+    product = product.reshape(2)
     return (forward_field, response, product)
 
 

time: 123 us -> 121 us (0.984)
  waiting for transfers between devices: 18 us -> 14.8 us
  Pallas kernels: 13.8 us -> 15.2 us
    ppermute x6, waiting for transfers between devices: 6.5 us -> 3.29 us  [on_device(): lax.ppermute(slab[far], 'seg', [(i, (i + far) % 4) for i in range(4)])]
    pallas_call x8 -> x10, Pallas kernels: 13.8 us -> 15.2 us  [run(): pl.pallas_call(kernel, in_specs=specs, out_specs=[pl.BlockSpec() if name...]
  transfers between devices with their start and end apart: 8 -> 8, of which waited for: 5 -> 6; matrix products, arithmetic and copies ran while one was open for 1% -> 1% of each run, Pallas kernels for 0% -> 2%
where the time goes in v3:
time: 121 us; the launch traced here: 120 us
  blocking collectives  64.9 us (54%)
  starting transfers between devices  23.4 us (19%)
  Pallas kernels  15.2 us (13%)
  waiting for transfers between devices  14.8 us (12%)
  local copies, waits for them, and re-layouts  1.27 us (1%)
    all_to_all x4, blocking collectives, exchange(): return lax.all_to_all(array, axis, split_axis=0, concat_axis=0, tiled=True)  64.9 us
    pallas_call x10, Pallas kernels, run(): pl.pallas_call(kernel, in_specs=specs, out_specs=[pl.BlockSpec() if name...  15.2 us
    all_to_all x1, waiting for transfers between devices, exchange(): return lax.all_to_all(array, axis, split_axis=0, concat_axis=0, tiled=True)  11.5 us
    ppermute x6, starting transfers between devices, on_device(): lax.ppermute(slab[far], 'seg', [(i, (i + far) % 4) for i in range(4)])  8.74 us
    all_to_all x1, starting transfers between devices, exchange(): return lax.all_to_all(array, axis, split_axis=0, concat_axis=0, tiled=True)  8.23 us
    ppermute x1, starting transfers between devices, on_device(): from_near = lax.ppermute(to_near, ALL, outward)  6.45 us
    ppermute x6, waiting for transfers between devices, on_device(): lax.ppermute(slab[far], 'seg', [(i, (i + far) % 4) for i in range(4)])  3.29 us
  transfers between devices with their start and end apart: 8, of which 6 were waited for; matrix products, arithmetic and copies ran while one was open for 1% of the time, Pallas kernels for 2%

profile of v3, /device:TPU:1, one launch (start us, length us, event | category | flops | bytes accessed | tf_op | source)
XLA Modules:
  0.0 120.4 jit_solution(4619005272078878937)
XLA Ops:
  0.6 0.1 pad_add_fusion.place_ref
  0.7 1.6 %prepare.1 = (f32[160,128]{1,0:T(8,128)S(1)}, f32[160,128]{1,0:T(8,128)S(1)}, f32[160,128]{1,0:T(8,128)S(1)}, f32[160,128]{1,0:T(8,128)S(1)}, f32[64,128]{1,0:T(8,128)S(1)}, /*index=5*/s32[1,256]{1,0:T(1,128)S(1)}) custom-call(s32[2]{0:T(128)S(1)} %pad_add_fusion.place_ref, f32[64,512]{1,0:T(8,128)} %k_ref.1, f32[64,512]{1,0:T(8,128)} %f_ref.1, ...), custom_call_target="tpu_custom_call" | custom-call | tf_op jit(solution)/shard_map/prepare/pallas_call | solution.py:571
  2.3 2.2 %collective-permute-start = (f32[160,128]{1,0:T(8,128)S(1)}, f32[160,128]{1,0:T(8,128)S(1)}, u32[]{:S(2)}, u32[]{:S(2)}) collective-permute-start(f32[160,128]{1,0:T(8,128)S(1)} %get-tuple-element.31), channel_id=1, source_target_pairs={{0,64},{64,128},{128,192},{192,0},{1,65},{65,129},{129,193},{193,1... | collective-permute-start | bytes 245768 | tf_op jit(solution)/shard_map/ppermute | solution.py:623
  4.5 2.6 %collective-permute-start.1 = (f32[160,128]{1,0:T(8,128)S(1)}, f32[160,128]{1,0:T(8,128)S(1)}, u32[]{:S(2)}, u32[]{:S(2)}) collective-permute-start(f32[160,128]{1,0:T(8,128)S(1)} %get-tuple-element.32), channel_id=1, source_target_pairs={{0,128},{64,192},{128,0},{192,64},{1,129},{65,193},{129,1},{193,65... | collective-permute-start | bytes 245768 | tf_op jit(solution)/shard_map/ppermute | solution.py:623
  7.2 1.1 collective-permute-start.2
  8.2 1.7 %load.1.tile = f32[3,512,128]{2,1,0:T(8,128)S(1)} custom-call(s32[2]{0:T(128)S(1)} %pad_add_fusion.place_ref, f32[512,512]{1,0:T(8,128)} %modes_ref.1, f32[160,128]{1,0:T(8,128)S(1)} %get-tuple-element.30.after_ref.slab_0), custom_call_target="tpu_custom_call" | custom-call | tf_op jit(solution)/shard_map/load/pallas_call | solution.py:571
  9.9 0.0 collective-permute-done.slab_1
  9.9 0.6 collective-permute-done.1.slab_2
  10.5 0.3 collective-permute-done.2.slab_3
  10.7 1.2 border.1
  12.0 6.5 %collective-permute-start.3 = (f32[128,128]{1,0:T(8,128)S(1)}, f32[128,128]{1,0:T(8,128)S(1)}, u32[]{:S(2)}, u32[]{:S(2)}) collective-permute-start(f32[128,128]{1,0:T(8,128)S(1)} %get-tuple-element.35), channel_id=1, source_target_pairs={{192,1},{193,2},{194,3},{195,4},{196,5},{197,6},{198,7},{199,8},{2... | collective-permute-start | bytes 196616 | tf_op jit(solution)/shard_map/ppermute | solution.py:632
  18.4 20.5 %all_to_all.25 = f32[64,1,128]{2,1,0:T(1,128)S(1)} all-to-all(f32[64,1,128]{2,1,0:T(1,128)S(1)} %bitcast.24), channel_id=1, replica_groups=mesh['seg'=4,'sub'=64] {'sub'}, dimensions={0} | all-to-all | bytes 65536 | tf_op jit(solution)/shard_map/all_to_all | solution.py:583
  38.9 0.0 collective-permute-done.3.near_ref
  38.9 3.4 %forward.1 = (f32[256,128]{1,0:T(8,128)S(1)}, f32[4,32,8,128]{3,2,1,0:T(8,128)S(1)}, s32[2,128]{1,0:T(2,128)S(1)}) custom-call(s32[2]{0:T(128)S(1)} %pad_add_fusion.place_ref, f32[160,128]{1,0:T(8,128)S(1)} %get-tuple-element.30.after_ref.slab_0, f32[160,128]{1,0:T(8,128)S(1)} %collective-permute-done.slab_1, f32[160,128]{1,0:T(8,128)S(1)} %collective-permute-done.1.slab_2, ...), custom_call_target="tpu_custom_call" | custom-call | tf_op jit(solution)/shard_map/forward/pallas_call | solution.py:571
  42.4 7.2 %all_to_all.26.in_ref = f32[4,64,128]{2,1,0:T(8,128)S(1)} all-to-all(f32[4,64,128]{2,1,0:T(8,128)S(1)} %bitcast.23), channel_id=1, replica_groups=mesh['seg'=4,'sub'=64] {'seg'}, dimensions={0} | all-to-all | bytes 262144 | tf_op jit(solution)/shard_map/all_to_all | solution.py:583
  49.6 0.7 pack.1
  50.3 0.0 copy-start
  50.3 0.0 copy-start.1
  50.3 18.3 %all_to_all.27 = f32[64,8,128]{2,1,0:T(8,128)S(1)} all-to-all(f32[64,8,128]{2,1,0:T(8,128)S(1)} %bitcast.22), channel_id=1, replica_groups=mesh['seg'=4,'sub'=64] {'sub'}, dimensions={0} | all-to-all | bytes 524288 | tf_op jit(solution)/shard_map/all_to_all | solution.py:583
  68.7 0.0 copy-done
  68.7 0.0 copy-done.1
  68.7 1.3 %voxels.1 = (f32[16,128]{1,0:T(8,128)S(1)}, f32[640,1,128]{2,1,0:T(1,128)S(1)}) custom-call(f32[512,128]{1,0:T(8,128)S(1)} %bitcast.18, f32[64,128]{1,0:T(8,128)S(1)} %bitcast.21, f32[16,128]{1,0:T(8,128)S(1)} %copy-done.1, f32[128,128]{1,0:T(8,128)S(1)} %copy-done), custom_call_target="tpu_custom_call" | custom-call | tf_op jit(solution)/shard_map/voxels/pallas_call | solution.py:571
  70.0 18.8 %all_to_all.28.in_ref = f32[640,1,128]{2,1,0:T(1,128)S(1)} all-to-all(f32[640,1,128]{2,1,0:T(1,128)S(1)} %get-tuple-element.43), channel_id=1, replica_groups=mesh['seg'=4,'sub'=64] {'sub'}, dimensions={0} | all-to-all | bytes 655360 | tf_op jit(solution)/shard_map/all_to_all | solution.py:583
  88.8 1.4 %driving.1 = (f32[80,128]{1,0:T(8,128)S(1)}, f32[80,128]{1,0:T(8,128)S(1)}, f32[80,128]{1,0:T(8,128)S(1)}, f32[80,128]{1,0:T(8,128)S(1)}) custom-call(s32[2]{0:T(128)S(1)} %pad_add_fusion.place_ref, s32[256]{0:T(256)S(1)} %bitcast.26, s32[2,128]{1,0:T(2,128)S(1)} %get-tuple-element.42.near_ref, f32[640,1,128]{2,1,0:T(1,128)S(1)} %all_to_all.28.in_ref), custom_call_target="tpu_custom_call" | custom-call | tf_op jit(solution)/shard_map/driving/pallas_call | solution.py:571
  90.2 0.4 collective-permute-start.4
  90.6 1.8 %collective-permute-start.5 = (f32[80,128]{1,0:T(8,128)S(1)}, f32[80,128]{1,0:T(8,128)S(1)}, u32[]{:S(2)}, u32[]{:S(2)}) collective-permute-start(f32[80,128]{1,0:T(8,128)S(1)} %get-tuple-element.46), channel_id=1, source_target_pairs={{0,128},{64,192},{128,0},{192,64},{1,129},{65,193},{129,1},{193,65... | collective-permute-start | bytes 122888 | tf_op jit(solution)/shard_map/ppermute | solution.py:669
  92.3 0.7 collective-permute-start.6
  93.0 0.1 stencils.1
  93.2 1.2 collective-permute-done.4.rest_1_
  94.3 0.6 collective-permute-done.5.rest_2_
  95.0 0.7 collective-permute-done.6.rest_3_
  95.6 3.2 %adjoint.1 = f32[256,128]{1,0:T(8,128)} custom-call(s32[2]{0:T(128)S(1)} %pad_add_fusion.place_ref, f32[3,512,128]{2,1,0:T(8,128)S(1)} %load.1.tile, f32[4,32,8,128]{3,2,1,0:T(8,128)S(1)} %get-tuple-element.41.kf_ref, f32[80,128]{1,0:T(8,128)S(1)} %get-tuple-element.44.after_ref.rest_0_, f32[80,128]{1,0:T(8,128)S(1)} %collective-permute-done.4.rest_1_, ...), custom_call_target="tpu_custom_call" | custom-call | tf_op jit(solution)/shard_map/adjoint/pallas_call | solution.py:571
  98.8 8.2 %all-to-all-start.4 = ((f32[256,1,128]{2,1,0:T(1,128)}), f32[256,1,128]{2,1,0:T(1,128)S(1)}, u32[]{:S(2)}, u32[]{:S(2)}) async-start(f32[256,1,128]{2,1,0:T(1,128)} %bitcast.13), calls=%async_computation.4 | async-start | bytes 262144 | tf_op jit(solution)/shard_map/all_to_all | solution.py:583
  107.1 0.7 copy.13
  107.7 0.6 copy.14
  108.3 11.5 %all-to-all-done.4 = f32[256,1,128]{2,1,0:T(1,128)S(1)} async-done(((f32[256,1,128]{2,1,0:T(1,128)}), f32[256,1,128]{2,1,0:T(1,128)S(1)}, u32[]{:S(2)}, u32[]{:S(2)}) %all-to-all-start.4) | async-done | bytes 131104 | tf_op jit(solution)/shard_map/all_to_all | solution.py:583
  119.9 0.6 total.1
Async XLA Ops:
  2.3 7.6 %collective-permute-start = (f32[160,128]{1,0:T(8,128)S(1)}, f32[160,128]{1,0:T(8,128)S(1)}, u32[]{:S(2)}, u32[]{:S(2)}) collective-permute-start(f32[160,128]{1,0:T(8,128)S(1)} %get-tuple-element.31), channel_id=1, source_target_pairs={{0,64},{64,128},{128,192},{192,0},{1,65},{65,129},{129,193},{193,1... | collective-permute-start | bytes 245768 | tf_op jit(solution)/shard_map/ppermute | solution.py:623
  4.5 5.9 %collective-permute-start.1 = (f32[160,128]{1,0:T(8,128)S(1)}, f32[160,128]{1,0:T(8,128)S(1)}, u32[]{:S(2)}, u32[]{:S(2)}) collective-permute-start(f32[160,128]{1,0:T(8,128)S(1)} %get-tuple-element.32), channel_id=1, source_target_pairs={{0,128},{64,192},{128,0},{192,64},{1,129},{65,193},{129,1},{193,65... | collective-permute-start | bytes 245768 | tf_op jit(solution)/shard_map/ppermute | solution.py:623
  7.2 3.6 %collective-permute-start.2 = (f32[160,128]{1,0:T(8,128)S(1)}, f32[160,128]{1,0:T(8,128)S(1)}, u32[]{:S(2)}, u32[]{:S(2)}) collective-permute-start(f32[160,128]{1,0:T(8,128)S(1)} %get-tuple-element.33), channel_id=1, source_target_pairs={{0,192},{64,0},{128,64},{192,128},{1,193},{65,1},{129,65},{193,129... | collective-permute-start | bytes 245768 | tf_op jit(solution)/shard_map/ppermute | solution.py:623
  12.0 27.0 %collective-permute-start.3 = (f32[128,128]{1,0:T(8,128)S(1)}, f32[128,128]{1,0:T(8,128)S(1)}, u32[]{:S(2)}, u32[]{:S(2)}) collective-permute-start(f32[128,128]{1,0:T(8,128)S(1)} %get-tuple-element.35), channel_id=1, source_target_pairs={{192,1},{193,2},{194,3},{195,4},{196,5},{197,6},{198,7},{199,8},{2... | collective-permute-start | bytes 196616 | tf_op jit(solution)/shard_map/ppermute | solution.py:632
  50.3 18.4 %copy-start = (f32[128,128]{1,0:T(8,128)S(1)}, f32[128,128]{1,0:T(8,128)}, u32[]{:S(2)}) copy-start(f32[128,128]{1,0:T(8,128)} %spread_ref.1) | copy-start | bytes 196612
  50.3 18.4 %copy-start.1 = (f32[16,128]{1,0:T(8,128)S(1)}, f32[16,128]{1,0:T(8,128)}, u32[]{:S(2)}) copy-start(f32[16,128]{1,0:T(8,128)} %weight_ref.1) | copy-start | bytes 24580
  90.2 4.1 %collective-permute-start.4 = (f32[80,128]{1,0:T(8,128)S(1)}, f32[80,128]{1,0:T(8,128)S(1)}, u32[]{:S(2)}, u32[]{:S(2)}) collective-permute-start(f32[80,128]{1,0:T(8,128)S(1)} %get-tuple-element.45), channel_id=1, source_target_pairs={{0,64},{64,128},{128,192},{192,0},{1,65},{65,129},{129,193},{193,1... | collective-permute-start | bytes 122888 | tf_op jit(solution)/shard_map/ppermute | solution.py:669
  90.6 4.4 %collective-permute-start.5 = (f32[80,128]{1,0:T(8,128)S(1)}, f32[80,128]{1,0:T(8,128)S(1)}, u32[]{:S(2)}, u32[]{:S(2)}) collective-permute-start(f32[80,128]{1,0:T(8,128)S(1)} %get-tuple-element.46), channel_id=1, source_target_pairs={{0,128},{64,192},{128,0},{192,64},{1,129},{65,193},{129,1},{193,65... | collective-permute-start | bytes 122888 | tf_op jit(solution)/shard_map/ppermute | solution.py:669
  92.3 3.3 %collective-permute-start.6 = (f32[80,128]{1,0:T(8,128)S(1)}, f32[80,128]{1,0:T(8,128)S(1)}, u32[]{:S(2)}, u32[]{:S(2)}) collective-permute-start(f32[80,128]{1,0:T(8,128)S(1)} %get-tuple-element.47), channel_id=1, source_target_pairs={{0,192},{64,0},{128,64},{192,128},{1,193},{65,1},{129,65},{193,129... | collective-permute-start | bytes 122888 | tf_op jit(solution)/shard_map/ppermute | solution.py:669
  98.8 21.0 %all-to-all-start.4 = ((f32[256,1,128]{2,1,0:T(1,128)}), f32[256,1,128]{2,1,0:T(1,128)S(1)}, u32[]{:S(2)}, u32[]{:S(2)}) async-start(f32[256,1,128]{2,1,0:T(1,128)} %bitcast.13), calls=%async_computation.4 | async-start | bytes 262144 | tf_op jit(solution)/shard_map/all_to_all | solution.py:583
